TPU v7x, 128 devices: a whole 4x4x4 slice. The times are simulated.
128 devices in a mesh: comm: 8 (over y, x_lo), dom: 16 (over z, x_hi, core).
Axes of the slice: x: 4 (x_hi: 2, x_lo: 2; x = x_hi * 2 + x_lo), y: 4, z: 4, core: 2. Of those that a mesh axis runs over, the one named last changes fastest.
Arguments:
- initial: bfloat16 [65536, 512], P(('comm', 'dom')), may hold values from -6 to 6
- held_cross: bfloat16 [65536, 512], P(('comm', 'dom')), may hold values from -6 to 6
- weights: bfloat16 [3, 512, 512], replicated, may hold values from -0.25 to 0.25
- need_rows: int32 [8, 16, 16, 1], P('comm', 'dom'), may hold values from 0 to 3
- tiles: bfloat16 [8, 16, 192, 128, 128], P('comm', 'dom'), may hold values from -1 to 1
- tile_scale: float32 [8, 16, 192], P('comm', 'dom'), may hold values from 0.01 to 0.1
- tile_src: int32 [8, 16, 192], P('comm', 'dom'), may hold values from 0 to 19, as said below
- tile_dst: int32 [8, 16, 192], P('comm', 'dom'), may hold values from 0 to 3
- tile_count: int32 [8, 16], P('comm', 'dom'), may hold values from 20 to 192
- cross_need: int32 [8, 16, 8, 2], P('comm', 'dom'), may hold values from 0 to 3
- cross_tiles: bfloat16 [8, 16, 64, 128, 128], P('comm', 'dom'), may hold values from -1 to 1
- cross_scale: float32 [8, 16, 64], P('comm', 'dom'), may hold values from 0.03 to 0.3
- cross_src: int32 [8, 16, 64], P('comm', 'dom'), may hold values from 0 to 15, as said below
- cross_dst: int32 [8, 16, 64], P('comm', 'dom'), may hold values from 0 to 3
Outputs:
- output: bfloat16 [65536, 512], P(('comm', 'dom'))
- refreshed: bfloat16 [65536, 512], P(('comm', 'dom'))
Inputs may be any that keep to these rules, and one draw needn't show every extreme that they name: `tile_src`: a partition's first 20 tiles name every in-community source index once. `cross_src`: a partition's first 16 cross tiles name every cross source index once.
All inputs are finite; a program needn't handle non-finite values.
Results may differ from a plain program's by a relative error of at most 0.0071.
Values may be sent and summed in bfloat16 or wider, within the bound.
A program may use at most 128 MiB of HBM per device.

v0:
```python
import math

import jax
import jax.numpy as jnp
from jax import lax
from jax.sharding import PartitionSpec as P

BLOCK = 128


ALPHA = 0.1
LAMBDA = 0.5


def dense_layer(total, initial, weight, level):
    beta = math.log(LAMBDA / level + 1.0)
    mixed = (1.0 - ALPHA) * total + ALPHA * initial.astype(jnp.float32)
    rounded = mixed.astype(jnp.bfloat16)
    turned = jnp.dot(rounded, weight, preferred_element_type=jnp.float32)
    return jax.nn.relu((1.0 - beta) * mixed + beta * turned).astype(jnp.bfloat16)


def placed(tile, scale, source, target, alive, blocks, sources):
    factor = jnp.where(alive, scale, jnp.zeros_like(scale))
    into = (target[:, None] == jnp.arange(blocks, dtype=jnp.int32)[None, :]).astype(
        jnp.float32
    ) * factor[:, None]
    where = (source[:, None] == jnp.arange(sources, dtype=jnp.int32)[None, :]).astype(jnp.float32)
    return jnp.einsum(
        "tb,ts,tij->bisj", into, where, tile.astype(jnp.float32), precision=lax.Precision.HIGHEST
    )


def assemble(tile, scale, source, target, live, blocks, sources):
    count = tile.shape[0]
    edge = tile.shape[1]
    alive = jnp.arange(count, dtype=jnp.int32) < live
    dense = placed(tile, scale, source, target, alive, blocks, sources)
    return dense.reshape(blocks * edge, sources * edge).astype(jnp.bfloat16)


def per_device(
    initial,
    held_cross,
    weights,
    need_rows,
    tiles,
    tile_scale,
    tile_src,
    tile_dst,
    tile_count,
    cross_need,
    cross_tiles,
    cross_scale,
    cross_src,
    cross_dst,
):
    width = initial.shape[1]
    rows = initial.shape[0]
    blocks = rows // BLOCK
    members = lax.axis_size("dom")
    groups = lax.axis_size("comm")
    need = need_rows[0, 0]
    spare = need.shape[1]
    live = tile_count[0, 0]
    inner_count = blocks + members * spare
    asked = lax.all_to_all(need_rows, "dom", split_axis=2, concat_axis=2, tiled=True)[0, 0].reshape(
        -1
    )

    def fetch(hidden):
        table = hidden.reshape(blocks, BLOCK, width)
        outgoing = table[asked].reshape(members, spare, BLOCK, width)
        incoming = lax.all_to_all(outgoing, "dom", split_axis=0, concat_axis=0, tiled=True)
        return jnp.concatenate([table, incoming.reshape(members * spare, BLOCK, width)], 0)

    inner_matrix = assemble(
        tiles[0, 0], tile_scale[0, 0], tile_src[0, 0], tile_dst[0, 0], live, blocks, inner_count
    )

    def inner(hidden):
        stacked = fetch(hidden).reshape(inner_count * BLOCK, width)
        return jnp.dot(inner_matrix, stacked, preferred_element_type=jnp.float32)

    wanted = lax.all_to_all(cross_need, "comm", split_axis=2, concat_axis=2, tiled=True)[
        0, 0
    ].reshape(-1)
    extra = cross_need.shape[3]
    cross_count = groups * extra
    cross_matrix = assemble(
        cross_tiles[0, 0],
        cross_scale[0, 0],
        cross_src[0, 0],
        cross_dst[0, 0],
        cross_tiles.shape[2],
        blocks,
        cross_count,
    )
    held = held_cross.astype(jnp.float32)
    hidden = initial
    for level in (1, 2):
        hidden = dense_layer(inner(hidden) + held, initial, weights[level - 1], level)
    table = hidden.reshape(blocks, BLOCK, width)
    outgoing = table[wanted].reshape(groups, extra, BLOCK, width)
    incoming = lax.all_to_all(outgoing, "comm", split_axis=0, concat_axis=0, tiled=True).reshape(
        cross_count * BLOCK, width
    )
    refreshed = jnp.dot(cross_matrix, incoming, preferred_element_type=jnp.float32).astype(
        jnp.bfloat16
    )
    total = inner(hidden) + refreshed.astype(jnp.float32)
    output = dense_layer(total, initial, weights[2], 3)
    return (output, refreshed)


def solution(mesh):
    in_specs = (
        P(("comm", "dom"), None),
        P(("comm", "dom"), None),
        P(),
        P("comm", "dom", None, None),
        P("comm", "dom", None, None, None),
        P("comm", "dom", None),
        P("comm", "dom", None),
        P("comm", "dom", None),
        P("comm", "dom"),
        P("comm", "dom", None, None),
        P("comm", "dom", None, None, None),
        P("comm", "dom", None),
        P("comm", "dom", None),
        P("comm", "dom", None),
    )
    out_specs = (P(("comm", "dom"), None), P(("comm", "dom"), None))
    return jax.shard_map(
        per_device, mesh=mesh, in_specs=in_specs, out_specs=out_specs, check_vma=False
    )
```

profile of v0, /device:TPU:0, one launch (start us, length us, event | category | flops | bytes accessed | tf_op | source)
XLA Modules:
  0.0 178.0 jit_solution(13211353891922280822)
XLA Ops:
  1.4 15.4 %all_to_all.30 = s32[1,1,16,1]{3,1,0,2:T(1,128)S(1)} all-to-all(s32[1,1,16,1]{3,1,0,2:T(1,128)S(1)} %copy.30), channel_id=1, replica_groups=mesh['comm'=8,'dom'=16] {'dom'}, dimensions={2} | all-to-all | bytes 128 | tf_op jit(solution)/shard_map/all_to_all | solution.py:67
  17.1 3.1 %gather_fusion = bf16[16,128,512]{2,1,0:T(8,128)(2,1)} fusion(bf16[4,128,512]{2,1,0:T(8,128)(2,1)} %bitcast.104, s32[1024]{0:T(1024)S(1)} %pad_clamp_fusion.1), kind=kCustom, calls=%fused_computation | custom fusion | bytes 4194368 | tf_op jit(solution)/shard_map/gather | solution.py:73
  20.2 3.9 %all-to-all-start.1 = ((bf16[16,1,128,512]{3,2,1,0:T(8,128)(2,1)}), bf16[16,1,128,512]{3,2,1,0:T(8,128)(2,1)S(1)}, u32[]{:S(2)}, u32[]{:S(2)}) async-start(bf16[16,1,128,512]{3,2,1,0:T(8,128)(2,1)} %bitcast.112), calls=%async_computation.1 | async-start | bytes 4194304 | tf_op jit(solution)/shard_map/all_to_all | solution.py:74
  25.5 10.0 %fusion.9 = bf16[20,4,128,128]{3,0,2,1:T(8,128)(2,1)} fusion(bf16[192,128,128]{2,1,0:T(8,128)(2,1)} %bitcast.124, f32[192,4]{0,1:T(4,128)S(1)} %fusion.80, f32[192,20]{0,1:T(8,128)S(1)} %fusion.76), kind=kOutput, calls=%fused_computation.16 | convolution fusion | flops 3021224960 | bytes 8931328 | tf_op jit(solution)/shard_map/tb,ts,tij->bisj/dot_general | solution.py:29
  35.5 17.9 %all-to-all-done.1 = bf16[16,1,128,512]{3,2,1,0:T(8,128)(2,1)S(1)} async-done(((bf16[16,1,128,512]{3,2,1,0:T(8,128)(2,1)}), bf16[16,1,128,512]{3,2,1,0:T(8,128)(2,1)S(1)}, u32[]{:S(2)}, u32[]{:S(2)}) %all-to-all-start.1) | async-done | bytes 2097184 | tf_op jit(solution)/shard_map/all_to_all | solution.py:74
  53.3 4.7 %all-to-all-start.4 = ((s32[1,1,8,2]{3,1,0,2:T(1,128)}), s32[1,1,8,2]{3,1,0,2:T(1,128)S(1)}, u32[]{:S(2)}, u32[]{:S(2)}) async-start(s32[1,1,8,2]{3,1,0,2:T(1,128)} %copy.32), calls=%async_computation.4 | async-start | bytes 8192 | tf_op jit(solution)/shard_map/all_to_all | solution.py:85
  60.1 1.6 fusion.44
  61.6 1.5 fusion.58
  63.1 2.0 %gather_fusion.1 = bf16[16,128,512]{2,1,0:T(8,128)(2,1)} fusion(bf16[4,128,512]{2,1,0:T(8,128)(2,1)S(1)} %bitcast.106, s32[1024]{0:T(1024)S(1)} %pad_clamp_fusion.1), kind=kCustom, calls=%fused_computation.1 | custom fusion | bytes 4194368 | tf_op jit(solution)/shard_map/gather | solution.py:73
  65.2 3.7 %all-to-all-start.2 = ((bf16[16,1,128,512]{3,2,1,0:T(8,128)(2,1)}), bf16[16,1,128,512]{3,2,1,0:T(8,128)(2,1)S(1)}, u32[]{:S(2)}, u32[]{:S(2)}) async-start(bf16[16,1,128,512]{3,2,1,0:T(8,128)(2,1)} %bitcast.110), calls=%async_computation.2 | async-start | bytes 4194304 | tf_op jit(solution)/shard_map/all_to_all | solution.py:74
  70.2 28.0 %all-to-all-done.2 = bf16[16,1,128,512]{3,2,1,0:T(8,128)(2,1)S(1)} async-done(((bf16[16,1,128,512]{3,2,1,0:T(8,128)(2,1)}), bf16[16,1,128,512]{3,2,1,0:T(8,128)(2,1)S(1)}, u32[]{:S(2)}, u32[]{:S(2)}) %all-to-all-start.2) | async-done | bytes 2097184 | tf_op jit(solution)/shard_map/all_to_all | solution.py:74
  100.2 1.6 fusion.52
  101.8 1.5 fusion.59
  103.3 2.0 %gather_fusion.3 = bf16[16,128,512]{2,1,0:T(8,128)(2,1)} fusion(bf16[4,128,512]{2,1,0:T(8,128)(2,1)S(1)} %bitcast.101, s32[1024]{0:T(1024)S(1)} %pad_clamp_fusion), kind=kCustom, calls=%fused_computation.3 | custom fusion | bytes 4194368 | tf_op jit(solution)/shard_map/gather | solution.py:104
  105.3 5.9 %all-to-all-start.5 = ((bf16[8,2,128,512]{3,2,1,0:T(8,128)(2,1)}), bf16[8,2,128,512]{3,2,1,0:T(8,128)(2,1)S(1)}, u32[]{:S(2)}, u32[]{:S(2)}) async-start(bf16[8,2,128,512]{3,2,1,0:T(8,128)(2,1)} %bitcast.33), calls=%async_computation.5 | async-start | bytes 4194304 | tf_op jit(solution)/shard_map/all_to_all | solution.py:105
  111.2 2.0 %gather_fusion.2 = bf16[16,128,512]{2,1,0:T(8,128)(2,1)} fusion(bf16[4,128,512]{2,1,0:T(8,128)(2,1)S(1)} %bitcast.102, s32[1024]{0:T(1024)S(1)} %pad_clamp_fusion.1), kind=kCustom, calls=%fused_computation.2 | custom fusion | bytes 4194368 | tf_op jit(solution)/shard_map/gather | solution.py:73
  113.2 24.6 %all-to-all-done.5 = bf16[8,2,128,512]{3,2,1,0:T(8,128)(2,1)S(1)} async-done(((bf16[8,2,128,512]{3,2,1,0:T(8,128)(2,1)}), bf16[8,2,128,512]{3,2,1,0:T(8,128)(2,1)S(1)}, u32[]{:S(2)}, u32[]{:S(2)}) %all-to-all-start.5) | async-done | bytes 2097184 | tf_op jit(solution)/shard_map/all_to_all | solution.py:105
  139.2 3.9 %all-to-all-start.3 = ((bf16[16,1,128,512]{3,2,1,0:T(8,128)(2,1)}), bf16[16,1,128,512]{3,2,1,0:T(8,128)(2,1)S(1)}, u32[]{:S(2)}, u32[]{:S(2)}) async-start(bf16[16,1,128,512]{3,2,1,0:T(8,128)(2,1)} %bitcast.21), calls=%async_computation.3 | async-start | bytes 4194304 | tf_op jit(solution)/shard_map/all_to_all | solution.py:74
  143.2 4.4 %fusion.18 = bf16[16,4,128,128]{3,0,2,1:T(8,128)(2,1)S(1)} fusion(bf16[64,128,128]{2,1,0:T(8,128)(2,1)} %bitcast.117, f32[64,4]{0,1:T(4,128)S(1)} %fusion.81, f32[64,16]{0,1:T(8,128)S(1)} %fusion.79), kind=kOutput, calls=%fused_computation.23 | convolution fusion | flops 806359040 | bytes 4199424 | tf_op jit(solution)/shard_map/tb,ts,tij->bisj/dot_general | solution.py:29
  147.5 2.1 %fusion.55 = bf16[512,512]{1,0:T(8,128)(2,1)} fusion(bf16[2048,512]{1,0:T(8,128)(2,1)S(1)} %bitcast.116, bf16[64,8,16,128]{3,2,1,0:T(8,128)(2,1)S(1)} %bitcast.118), kind=kOutput, calls=%fused_computation.45 | convolution fusion | flops 1074003968 | bytes 4718592 | tf_op jit(solution)/shard_map/dot_general | solution.py:108
  149.6 22.6 %all-to-all-done.3 = bf16[16,1,128,512]{3,2,1,0:T(8,128)(2,1)S(1)} async-done(((bf16[16,1,128,512]{3,2,1,0:T(8,128)(2,1)}), bf16[16,1,128,512]{3,2,1,0:T(8,128)(2,1)S(1)}, u32[]{:S(2)}, u32[]{:S(2)}) %all-to-all-start.3) | async-done | bytes 2097184 | tf_op jit(solution)/shard_map/all_to_all | solution.py:74
  172.4 1.7 copy-done.14
  174.1 1.6 fusion.36
  175.7 2.3 %fusion.60 = bf16[512,512]{1,0:T(8,128)(2,1)} fusion(f32[512,512]{1,0:T(8,128)S(1)} %fusion.36, bf16[3,512,512]{2,1,0:T(8,128)(2,1)} %param.16), kind=kOutput, calls=%fused_computation.48 | convolution fusion | flops 270008320 | bytes 3145728 | tf_op jit(solution)/shard_map/dot_general | solution.py:19
  (51 shorter events, 8.9 us)
Async XLA Ops:
  20.2 4.5 %copy-start.3 = (s32[1,1,8,2]{2,3,1,0:T(2,128)S(1)}, s32[1,1,8,2]{2,3,1,0:T(2,128)}, u32[]{:S(2)}) copy-start(s32[1,1,8,2]{2,3,1,0:T(2,128)} %param.23) | copy-start | bytes 196
  20.2 5.2 %copy-start.5 = (f32[1,1,192]{2,1,0:T(1,128)S(1)}, f32[1,1,192]{2,1,0:T(1,128)}, u32[]{:S(2)}) copy-start(f32[1,1,192]{2,1,0:T(1,128)} %param.19) | copy-start | bytes 2308
  20.2 5.2 %copy-start.6 = (s32[1,1,192]{2,1,0:T(1,128)S(1)}, s32[1,1,192]{2,1,0:T(1,128)}, u32[]{:S(2)}) copy-start(s32[1,1,192]{2,1,0:T(1,128)} %param.21) | copy-start | bytes 2308
  20.2 5.2 %copy-start.4 = (s32[1,1,192]{2,1,0:T(1,128)S(1)}, s32[1,1,192]{2,1,0:T(1,128)}, u32[]{:S(2)}) copy-start(s32[1,1,192]{2,1,0:T(1,128)} %param.20) | copy-start | bytes 2308
  20.2 33.1 %all-to-all-start.1 = ((bf16[16,1,128,512]{3,2,1,0:T(8,128)(2,1)}), bf16[16,1,128,512]{3,2,1,0:T(8,128)(2,1)S(1)}, u32[]{:S(2)}, u32[]{:S(2)}) async-start(bf16[16,1,128,512]{3,2,1,0:T(8,128)(2,1)} %bitcast.112), calls=%async_computation.1 | async-start | bytes 4194304 | tf_op jit(solution)/shard_map/all_to_all | solution.py:74
  25.5 32.5 %copy-start = (bf16[512,512]{1,0:T(8,128)(2,1)S(1)}, bf16[512,512]{1,0:T(8,128)(2,1)}, u32[]{:S(2)}) copy-start(bf16[512,512]{1,0:T(8,128)(2,1)} %param.14) | copy-start | bytes 1572868
  53.3 11.9 %all-to-all-start.4 = ((s32[1,1,8,2]{3,1,0,2:T(1,128)}), s32[1,1,8,2]{3,1,0,2:T(1,128)S(1)}, u32[]{:S(2)}, u32[]{:S(2)}) async-start(s32[1,1,8,2]{3,1,0,2:T(1,128)} %copy.32), calls=%async_computation.4 | async-start | bytes 8192 | tf_op jit(solution)/shard_map/all_to_all | solution.py:85
  58.0 1.0 copy-start.9
  58.0 2.1 %copy-start.12 = (bf16[20,4,128,128]{3,0,2,1:T(8,128)(2,1)S(1)}, bf16[20,4,128,128]{3,0,2,1:T(8,128)(2,1)}, u32[]{:S(2)}) copy-start(bf16[20,4,128,128]{3,0,2,1:T(8,128)(2,1)} %fusion.9) | copy-start | bytes 7864324
  65.2 33.0 %all-to-all-start.2 = ((bf16[16,1,128,512]{3,2,1,0:T(8,128)(2,1)}), bf16[16,1,128,512]{3,2,1,0:T(8,128)(2,1)S(1)}, u32[]{:S(2)}, u32[]{:S(2)}) async-start(bf16[16,1,128,512]{3,2,1,0:T(8,128)(2,1)} %bitcast.110), calls=%async_computation.2 | async-start | bytes 4194304 | tf_op jit(solution)/shard_map/all_to_all | solution.py:74
  98.2 1.0 copy-start.10
  98.2 2.1 %copy-start.13 = (bf16[20,4,128,128]{3,0,2,1:T(8,128)(2,1)S(1)}, bf16[20,4,128,128]{3,0,2,1:T(8,128)(2,1)}, u32[]{:S(2)}) copy-start(bf16[20,4,128,128]{3,0,2,1:T(8,128)(2,1)} %fusion.9) | copy-start | bytes 7864324
  105.3 32.5 %all-to-all-start.5 = ((bf16[8,2,128,512]{3,2,1,0:T(8,128)(2,1)}), bf16[8,2,128,512]{3,2,1,0:T(8,128)(2,1)S(1)}, u32[]{:S(2)}, u32[]{:S(2)}) async-start(bf16[8,2,128,512]{3,2,1,0:T(8,128)(2,1)} %bitcast.33), calls=%async_computation.5 | async-start | bytes 4194304 | tf_op jit(solution)/shard_map/all_to_all | solution.py:105
  137.8 1.3 copy-start.1
  137.8 5.3 %copy-start.11 = (f32[1,1,64]{2,1,0:T(1,128)S(1)}, f32[1,1,64]{2,1,0:T(1,128)}, u32[]{:S(2)}) copy-start(f32[1,1,64]{2,1,0:T(1,128)} %param.25) | copy-start | bytes 772
  137.8 5.3 %copy-start.8 = (s32[1,1,64]{2,1,0:T(1,128)S(1)}, s32[1,1,64]{2,1,0:T(1,128)}, u32[]{:S(2)}) copy-start(s32[1,1,64]{2,1,0:T(1,128)} %param.27) | copy-start | bytes 772
  137.8 5.3 %copy-start.7 = (s32[1,1,64]{2,1,0:T(1,128)S(1)}, s32[1,1,64]{2,1,0:T(1,128)}, u32[]{:S(2)}) copy-start(s32[1,1,64]{2,1,0:T(1,128)} %param.26) | copy-start | bytes 772
  139.2 33.0 %all-to-all-start.3 = ((bf16[16,1,128,512]{3,2,1,0:T(8,128)(2,1)}), bf16[16,1,128,512]{3,2,1,0:T(8,128)(2,1)S(1)}, u32[]{:S(2)}, u32[]{:S(2)}) async-start(bf16[16,1,128,512]{3,2,1,0:T(8,128)(2,1)} %bitcast.21), calls=%async_computation.3 | async-start | bytes 4194304 | tf_op jit(solution)/shard_map/all_to_all | solution.py:74
  143.2 4.4 %copy-start.2 = (bf16[8,2,128,512]{3,2,1,0:T(8,128)(2,1)S(1)}, bf16[8,2,128,512]{3,2,1,0:T(8,128)(2,1)}, u32[]{:S(2)}) copy-start(bf16[8,2,128,512]{3,2,1,0:T(8,128)(2,1)} %copy-done.1) | copy-start | bytes 6291460
  172.1 1.9 %copy-start.14 = (bf16[20,4,128,128]{3,0,2,1:T(8,128)(2,1)S(1)}, bf16[20,4,128,128]{3,0,2,1:T(8,128)(2,1)}, u32[]{:S(2)}) copy-start(bf16[20,4,128,128]{3,0,2,1:T(8,128)(2,1)} %fusion.9) | copy-start | bytes 7864324
  172.1 2.0 %copy-start.15 = (bf16[512,512]{1,0:T(8,128)(2,1)S(1)}, bf16[512,512]{1,0:T(8,128)(2,1)}, u32[]{:S(2)}) copy-start(bf16[512,512]{1,0:T(8,128)(2,1)} %fusion.55) | copy-start | bytes 1572868
where the time goes:
time: 179 us; the launch traced here: 178 us
  waiting for transfers between devices  93 us (52%)
  matrix products  26.4 us (15%)
  starting transfers between devices  22 us (12%)
  local copies, waits for them, and re-layouts  18 us (10%)
  blocking collectives  15.4 us (9%)
    all_to_all x3, waiting for transfers between devices, fetch(): lax.all_to_all(outgoing, 'dom', split_axis=0, concat_axis=0, tiled=True)  68.4 us
    all_to_all x1, waiting for transfers between devices, per_device(): lax.all_to_all(outgoing, 'comm', split_axis=0, concat_axis=0, tiled=True)  24.6 us
    all_to_all x1, blocking collectives, per_device(): lax.all_to_all(need_rows, 'dom', split_axis=2, concat_axis=2, tiled=True)  15.4 us
    dot_general x2, matrix products, placed(): jnp.einsum('tb,ts,tij->bisj', into, where, tile.astype(jnp.float32), prec...  14.4 us
    all_to_all x3, starting transfers between devices, fetch(): lax.all_to_all(outgoing, 'dom', split_axis=0, concat_axis=0, tiled=True)  11.5 us
    unnamed x34, local copies, waits for them, and re-layouts  8.18 us
    gather x3, local copies, waits for them, and re-layouts, fetch(): outgoing = table[asked].reshape(members, spare, BLOCK, width)  7.15 us
    all_to_all x1, starting transfers between devices, per_device(): lax.all_to_all(outgoing, 'comm', split_axis=0, concat_axis=0, tiled=True)  5.86 us
  transfers between devices with their start and end apart: 5, of which 4 were waited for; matrix products, arithmetic and copies ran while one was open for 14% of the time, Pallas kernels for 0%

commit v1 on v0

v1 whole, which is shorter than its diff:
```python
import functools
import math

import jax
import jax.numpy as jnp
from jax import lax
from jax.experimental import pallas as pl
from jax.experimental.pallas import tpu as pltpu
from jax.sharding import PartitionSpec as P

BLOCK = 128
D = 512
ROWS = 512
TILES = 192
XTILES = 64
SOURCES = 20
XSOURCES = 16
ALPHA = 0.1
LAMBDA = 0.5
MESH = pl.DeviceIdType.MESH
BF = jnp.bfloat16
F32 = jnp.float32
I32 = jnp.int32
OWN, ANT = 0, 1


def pair(i):
    return pl.ds(i * 2, 2)


def chain_tables(key_ref, tbl_ref, halves, none, row):
    iota0 = lax.broadcasted_iota(I32, (BLOCK, BLOCK), 0)
    iota1 = lax.broadcasted_iota(I32, (BLOCK, BLOCK), 1)
    last = jnp.full((1, BLOCK), -1, I32)
    prev = [jnp.full((1, BLOCK), -1, I32) for _ in range(halves)]
    for h in range(halves):
        down = jnp.broadcast_to(key_ref[0:1, h * BLOCK : (h + 1) * BLOCK], (BLOCK, BLOCK)).T
        who = iota0 + h * BLOCK
        hit = jnp.where(down == iota1, who, -1)
        last = jnp.maximum(last, jnp.max(hit, axis=0, keepdims=True))
        for j in range(h, halves):
            across = jnp.broadcast_to(key_ref[0:1, j * BLOCK : (j + 1) * BLOCK], (BLOCK, BLOCK))
            same = jnp.logical_and(down == across, who < iota1 + j * BLOCK)
            prev[j] = jnp.maximum(prev[j], jnp.max(jnp.where(same, who, -1), axis=0, keepdims=True))
    tbl_ref[row : row + 1, 0:BLOCK] = jnp.where(last < 0, none, last)
    for j in range(halves):
        tbl_ref[row : row + 1, (j + 1) * BLOCK : (j + 2) * BLOCK] = jnp.where(prev[j] < 0, none, prev[j])


def kernel(
    init_hbm,
    held_hbm,
    weights_hbm,
    need_ref,
    tiles_hbm,
    scale_ref,
    src_ref,
    dst_ref,
    count_ref,
    xneed_ref,
    xtiles_hbm,
    xscale_ref,
    xsrc_ref,
    xdst_ref,
    out_ref,
    ref_ref,
    init,
    held,
    weights,
    tiles,
    slots,
    adj,
    xadj,
    acc,
    xacc,
    rounded,
    hbuf,
    rb,
    ant0,
    ant1,
    ant2,
    xf,
    zf,
    nbt,
    gb,
    cr,
    yf,
    gx,
    rq,
    reqs,
    xreqs,
    reqs_s,
    xreqs_s,
    keys,
    tbl,
    tbl_s,
    lsem,
    ssem,
    qsem,
    xs,
    as_,
    zs,
    rs,
    ns,
    ys,
    cs,
):
    comm = lax.axis_index("comm")
    dom = lax.axis_index("dom")
    y, xl = comm // 2, comm % 2
    z, xh, c = dom // 4, (dom // 2) % 2, dom % 2
    x = xh * 2 + xl

    def dev(px, py, pz, pc):
        return (py * 2 + px % 2, pz * 4 + (px // 2) * 2 + pc)

    xp, xm = (x + 1) % 4, (x + 3) % 4
    xnb = xh * 2 + (1 - xl)
    xot = (x + 3 + 2 * xl) % 4
    zp, zm, z2 = (z + 1) % 4, (z + 3) % 4, (z + 2) % 4
    yp, ym, y2 = (y + 1) % 4, (y + 3) % 4, (y + 2) % 4

    ant = (ant0, ant1, ant2)

    loads = {}

    def load(name, src, dst, i):
        loads[name] = pltpu.make_async_copy(src, dst, lsem.at[i])
        loads[name].start()

    load("init", init_hbm, init, 0)
    load("tiles0", tiles_hbm.at[pl.ds(0, 96)], tiles.at[pl.ds(0, 96)], 1)
    load("tiles1", tiles_hbm.at[pl.ds(96, 96)], tiles.at[pl.ds(96, 96)], 2)
    load("held", held_hbm, held, 3)
    load("weights", weights_hbm, weights, 4)

    barrier = pltpu.get_barrier_semaphore()
    peers = [
        dev(xp, y, z, c),
        dev(xm, y, z, c),
        dev(x, y, z, 1 - c),
        dev(x, y, zp, 0),
        dev(x, y, zp, 1),
        dev(x, y, zm, 0),
        dev(x, y, zm, 1),
        dev(x, y, z2, 0),
        dev(x, y, z2, 1),
        dev(x, yp, z, c),
        dev(x, ym, z, c),
        dev(x, y2, z, c),
    ]
    for peer in peers:
        pl.semaphore_signal(barrier, inc=1, device_id=peer, device_id_type=MESH)
    rq[0:1, 0:16] = need_ref[...]
    rq[1:2, 0:16] = xneed_ref[...]
    loads["init"].wait()
    pl.semaphore_wait(barrier, len(peers))

    sent = []

    def send(src, dst, sem, device):
        copy = pltpu.make_async_remote_copy(
            src_ref=src,
            dst_ref=dst,
            send_sem=ssem.at[len(sent)],
            recv_sem=sem,
            device_id=device,
            device_id_type=MESH,
        )
        copy.start()
        sent.append(copy)

    def arrived(dst, sem):
        pltpu.make_async_remote_copy(
            src_ref=dst,
            dst_ref=dst,
            send_sem=ssem.at[0],
            recv_sem=sem,
            device_id=dev(x, y, z, 1 - c),
            device_id_type=MESH,
        ).wait_recv()

    def x_first(e, table, half):
        if half == 0:
            for k in range(2):
                send(table.at[k], xf.at[e, 0, k], xs.at[e, 0, k], dev(xp, y, z, c))
        else:
            for k in range(2):
                send(table.at[2 + k], xf.at[e, 1, k], xs.at[e, 1, k], dev(xm, y, z, c))

    def x_forward(e, k):
        arrived(xf.at[e, 0, k], xs.at[e, 0, k])
        send(xf.at[e, 0, k], ant[e].at[k], as_.at[e, k], dev(xp, y, z, c))
        arrived(xf.at[e, 1, k], xs.at[e, 1, k])
        send(xf.at[e, 1, k], ant[e].at[2 + k], as_.at[e, 2 + k], dev(xm, y, z, c))

    def part(pz, ty, pc):
        return pz * 4 + (xh if ty == OWN else 1 - xh) * 2 + pc

    def z_send(e, ty, table):
        p = part(z, ty, c)

        def gather(g, pz, pc):
            want = reqs_s[pz * 2 + pc, 0, p]
            gb[ty, g] = table[want]
            return gb.at[ty, g]

        mine = rb.at[e, p]
        send(gather(0, z2, 0), zf.at[e, 0, ty], zs.at[e, 0, ty], dev(x, y, zp, c))
        send(gather(1, z2, 1), zf.at[e, 1, ty], zs.at[e, 1, ty], dev(x, y, zm, c))
        send(gather(2, zp, 0), mine, rs.at[e, 0, ty, c], dev(x, y, zp, 0))
        send(gather(3, zm, 0), mine, rs.at[e, 1, ty, c], dev(x, y, zm, 0))
        send(gather(4, zp, 1), mine, rs.at[e, 0, ty, c], dev(x, y, zp, 1))
        send(gather(5, zm, 1), mine, rs.at[e, 1, ty, c], dev(x, y, zm, 1))
        send(gather(6, z, 1 - c), mine, rs.at[e, 3, ty, 0], dev(x, y, z, 1 - c))
        want = reqs_s[z * 2 + c, 0, p]
        rb[e, p] = table[want]

    def z_forward(e, ty):
        arrived(zf.at[e, 0, ty], zs.at[e, 0, ty])
        send(zf.at[e, 0, ty], rb.at[e, part(zm, ty, c)], rs.at[e, 2, ty, c], dev(x, y, zp, 0))
        arrived(zf.at[e, 1, ty], zs.at[e, 1, ty])
        send(zf.at[e, 1, ty], rb.at[e, part(zp, ty, c)], rs.at[e, 2, ty, c], dev(x, y, zm, 1))

    def dot_into(total, lhs, rhs, first=False):
        @pl.loop(0, 2)
        def _(n):
            cols = pl.ds(pl.multiple_of(n * 256, 256), 256)
            value = jnp.dot(lhs[...], rhs[:, :, cols].reshape(256, 256), preferred_element_type=F32)
            if first:
                total[:, cols] = value
            else:
                total[:, cols] += value

    def dot_own(table):
        dot_into(acc, adj.at[0], table.at[pl.ds(0, 2)], first=True)
        dot_into(acc, adj.at[1], table.at[pl.ds(2, 2)])

    def dot_pair(e, ty, key):
        pz = (zm, zp, z2, z)[key]
        if key == 3:
            arrived(rb.at[e, part(z, ty, 1 - c)], rs.at[e, 3, ty, 0])
        else:
            for pc in range(2):
                arrived(rb.at[e, part(pz, ty, pc)], rs.at[e, key, ty, pc])
        j = pz * 2 + (xh if ty == OWN else 1 - xh)
        dot_into(acc, adj.at[2 + j], rb.at[e, pair(j)])

    def drain():
        for copy in sent:
            copy.wait_send()
        sent.clear()

    def layer(level, added, target, after=lambda half: None, blocks=True):
        beta = math.log(LAMBDA / level + 1.0)
        for half in range(2):
            rows = pl.ds(half * 256, 256)
            total = acc[rows, :] + added[rows, :].astype(F32)
            mixed = (1.0 - ALPHA) * total + ALPHA * init[2 * half : 2 * half + 2].reshape(256, D).astype(F32)
            acc[rows, :] = mixed
            rounded[rows, :] = mixed.astype(BF)
            for n in range(2):
                cols = pl.ds(n * 256, 256)
                turned = jnp.dot(rounded[rows, :], weights[level - 1, :, cols], preferred_element_type=F32)
                done = jax.nn.relu((1.0 - beta) * acc[rows, cols] + beta * turned).astype(BF)
                if blocks:
                    target[2 * half : 2 * half + 2, :, cols] = done.reshape(2, BLOCK, 256)
                else:
                    target[rows, cols] = done
            after(half)

    x_first(0, init, 0)
    x_first(0, init, 1)
    for pz in (zp, zm, z2):
        for pc in range(2):
            send(rq, reqs.at[z * 2 + c], qsem.at[z * 2 + c], dev(x, y, pz, pc))
    send(rq, reqs.at[z * 2 + c], qsem.at[z * 2 + c], dev(x, y, z, 1 - c))
    for py in (yp, ym, y2):
        send(rq, xreqs.at[y], qsem.at[8 + y], dev(x, py, z, c))
    reqs[z * 2 + c] = rq[...]
    xreqs[y] = rq[...]

    keys[...] = jnp.full((8, 256), -1, I32)
    live = count_ref[0, 0]
    at = lax.broadcasted_iota(I32, (1, TILES), 1)
    keys[0:1, 0:TILES] = jnp.where(at < live, dst_ref[...] * SOURCES + src_ref[...], -1)
    chain_tables(keys, tbl, 2, TILES, 0)
    keys[0:1, 0:256] = jnp.full((1, 256), -1, I32)
    keys[0:1, 0:XTILES] = xdst_ref[...] * XSOURCES + xsrc_ref[...]
    chain_tables(keys, tbl, 1, TILES, 1)
    copy_tbl = pltpu.make_async_copy(tbl, tbl_s, lsem.at[5])
    copy_tbl.start()
    slots[TILES] = jnp.zeros((BLOCK, BLOCK), F32)

    for pz in (zp, zm, z2):
        for pc in range(2):
            arrived(reqs.at[pz * 2 + pc], qsem.at[pz * 2 + pc])
    arrived(reqs.at[z * 2 + 1 - c], qsem.at[z * 2 + 1 - c])
    copy_req = pltpu.make_async_copy(reqs, reqs_s, lsem.at[6])
    copy_req.start()
    copy_req.wait()
    z_send(0, OWN, init)
    for py in (yp, ym, y2):
        arrived(xreqs.at[py], qsem.at[8 + py])
    copy_xreq = pltpu.make_async_copy(xreqs, xreqs_s, lsem.at[7])
    copy_xreq.start()
    copy_xreq.wait()
    copy_tbl.wait()

    def chain(tile_ref, scales, row, start, stop):
        @pl.loop(start, stop)
        def _(t):
            before = tbl_s[row, BLOCK + t]
            slots[t] = slots[before] + scales[0, t] * tile_ref[t].astype(F32)

    def place(target, row, sources):
        @pl.loop(0, sources // 2)
        def _(s2):
            for b in range(4):
                for s in range(2):
                    final = tbl_s[row, b * sources + s2 * 2 + s]
                    target[s2, b * BLOCK : (b + 1) * BLOCK, s * BLOCK : (s + 1) * BLOCK] = slots[final].astype(BF)

    loads["tiles0"].wait()
    chain(tiles, scale_ref, 0, 0, 48)
    x_forward(0, 0)
    chain(tiles, scale_ref, 0, 48, 96)
    x_forward(0, 1)
    loads["tiles1"].wait()
    chain(tiles, scale_ref, 0, 96, 144)
    z_forward(0, OWN)
    chain(tiles, scale_ref, 0, 144, 192)
    load("xtiles", xtiles_hbm, tiles.at[pl.ds(0, XTILES)], 8)
    place(adj, 0, SOURCES)
    dot_own(init)
    for k in range(4):
        arrived(ant[0].at[k], as_.at[0, k])
    z_send(0, ANT, ant[0])
    dot_pair(0, OWN, 3)
    dot_pair(0, OWN, 0)
    dot_pair(0, OWN, 1)
    z_forward(0, ANT)
    dot_pair(0, OWN, 2)
    loads["xtiles"].wait()
    chain(tiles, xscale_ref, 1, 0, XTILES)
    place(xadj, 1, XSOURCES)
    loads["held"].wait()
    loads["weights"].wait()
    dot_pair(0, ANT, 3)
    dot_pair(0, ANT, 0)
    dot_pair(0, ANT, 1)
    dot_pair(0, ANT, 2)
    drain()
    layer(1, held, hbuf.at[0], lambda half: x_first(1, hbuf.at[0], half))

    h1 = hbuf.at[0]
    z_send(1, OWN, h1)
    dot_own(h1)
    x_forward(1, 0)
    x_forward(1, 1)
    z_forward(1, OWN)
    dot_pair(1, OWN, 3)
    dot_pair(1, OWN, 0)
    dot_pair(1, OWN, 1)
    for k in range(4):
        arrived(ant[1].at[k], as_.at[1, k])
    z_send(1, ANT, ant[1])
    dot_pair(1, OWN, 2)
    dot_pair(1, ANT, 3)
    z_forward(1, ANT)
    dot_pair(1, ANT, 0)
    dot_pair(1, ANT, 1)
    dot_pair(1, ANT, 2)
    drain()

    h2 = hbuf.at[1]

    def x_table(half):
        for k in range(2 * half, 2 * half + 2):
            send(h2.at[k], nbt.at[k], ns.at[k], dev(xnb, y, z, c))

    def x_table_forward(k):
        arrived(nbt.at[k], ns.at[k])
        send(nbt.at[k], ant[2].at[k], as_.at[2, k], dev(xot, y, z, c))

    def group(py, ty):
        return py * 2 + (xl if ty == OWN else 1 - xl)

    def y_send(ty, table):
        me = group(y, ty)

        def gather(g, py, k):
            want = xreqs_s[py, 1, me * 2 + k]
            gx[ty, g] = table[want]

        gather(0, y2, 0)
        gather(1, y2, 1)
        send(gx.at[ty, 0], yf.at[0, ty], ys.at[0, ty], dev(x, yp, z, c))
        send(gx.at[ty, 1], yf.at[1, ty], ys.at[1, ty], dev(x, ym, z, c))
        mine = cr.at[pair(me)]
        for i, py in enumerate((yp, ym)):
            gather(2 + 2 * i, py, 0)
            gather(3 + 2 * i, py, 1)
            send(gx.at[ty, pair(1 + i)], mine, cs.at[i, ty], dev(x, py, z, c))
        for k in range(2):
            want = xreqs_s[y, 1, me * 2 + k]
            cr[me * 2 + k] = table[want]

    def y_forward(ty):
        arrived(yf.at[0, ty], ys.at[0, ty])
        send(yf.at[0, ty], cr.at[group(ym, ty) * 2], cs.at[2, ty], dev(x, yp, z, c))
        arrived(yf.at[1, ty], ys.at[1, ty])
        send(yf.at[1, ty], cr.at[group(yp, ty) * 2 + 1], cs.at[3, ty], dev(x, ym, z, c))

    layer(2, held, h2, x_table)
    z_send(2, OWN, h2)
    y_send(OWN, h2)
    dot_own(h2)
    x_table_forward(0)
    z_forward(2, OWN)
    y_forward(OWN)
    x_table_forward(1)
    dot_pair(2, OWN, 3)
    x_table_forward(2)
    dot_pair(2, OWN, 0)
    dot_pair(2, OWN, 1)
    x_table_forward(3)
    y_send(ANT, nbt)

    def cross_dot(ty, key, first=False):
        py = (ym, yp, y2, y)[key]
        g = group(py, ty)
        if key < 2:
            arrived(cr.at[pair(g)], cs.at[key, ty])
        if key == 2:
            arrived(cr.at[g * 2], cs.at[2, ty])
            arrived(cr.at[g * 2 + 1], cs.at[3, ty])
        dot_into(xacc, xadj.at[g], cr.at[pair(g)], first)

    cross_dot(OWN, 3, first=True)
    cross_dot(ANT, 3)
    dot_pair(2, OWN, 2)
    cross_dot(OWN, 0)
    cross_dot(OWN, 1)
    for k in range(4):
        arrived(ant[2].at[k], as_.at[2, k])
    z_send(2, ANT, ant[2])
    cross_dot(OWN, 2)
    y_forward(ANT)
    dot_pair(2, ANT, 3)
    z_forward(2, ANT)
    cross_dot(ANT, 0)
    cross_dot(ANT, 1)
    cross_dot(ANT, 2)
    ref_ref[...] = xacc[...].astype(BF)
    dot_pair(2, ANT, 0)
    dot_pair(2, ANT, 1)
    dot_pair(2, ANT, 2)
    layer(3, ref_ref, out_ref, blocks=False)
    drain()


def per_device(
    initial,
    held_cross,
    weights,
    need_rows,
    tiles,
    tile_scale,
    tile_src,
    tile_dst,
    tile_count,
    cross_need,
    cross_tiles,
    cross_scale,
    cross_src,
    cross_dst,
):
    hbm = pl.BlockSpec(memory_space=pl.ANY)
    vmem = pl.BlockSpec(memory_space=pltpu.VMEM)
    smem = pl.BlockSpec(memory_space=pltpu.SMEM)
    dma = pltpu.SemaphoreType.DMA
    table = jax.ShapeDtypeStruct((ROWS, D), BF)
    out = pl.pallas_call(
        kernel,
        out_shape=(table, table),
        in_specs=[hbm, hbm, hbm, vmem, hbm, smem, vmem, vmem, smem, vmem, hbm, smem, vmem, vmem],
        out_specs=(vmem, vmem),
        scratch_shapes=[
            pltpu.VMEM((4, BLOCK, D), BF),
            pltpu.VMEM((ROWS, D), BF),
            pltpu.VMEM((3, D, D), BF),
            pltpu.VMEM((TILES, BLOCK, BLOCK), BF),
            pltpu.VMEM((TILES + 1, BLOCK, BLOCK), F32),
            pltpu.VMEM((SOURCES // 2, ROWS, 2 * BLOCK), BF),
            pltpu.VMEM((XSOURCES // 2, ROWS, 2 * BLOCK), BF),
            pltpu.VMEM((ROWS, D), F32),
            pltpu.VMEM((ROWS, D), F32),
            pltpu.VMEM((ROWS, D), BF),
            pltpu.VMEM((2, 4, BLOCK, D), BF),
            pltpu.VMEM((3, 16, BLOCK, D), BF),
            pltpu.VMEM((4, BLOCK, D), BF),
            pltpu.VMEM((4, BLOCK, D), BF),
            pltpu.VMEM((4, BLOCK, D), BF),
            pltpu.VMEM((2, 2, 2, BLOCK, D), BF),
            pltpu.VMEM((3, 2, 2, BLOCK, D), BF),
            pltpu.VMEM((4, BLOCK, D), BF),
            pltpu.VMEM((2, 7, BLOCK, D), BF),
            pltpu.VMEM((16, BLOCK, D), BF),
            pltpu.VMEM((2, 2, BLOCK, D), BF),
            pltpu.VMEM((2, 6, BLOCK, D), BF),
            pltpu.VMEM((8, BLOCK), I32),
            pltpu.VMEM((8, 8, BLOCK), I32),
            pltpu.VMEM((4, 8, BLOCK), I32),
            pltpu.SMEM((8, 8, BLOCK), I32),
            pltpu.SMEM((4, 8, BLOCK), I32),
            pltpu.VMEM((8, 2 * BLOCK), I32),
            pltpu.VMEM((8, 3 * BLOCK), I32),
            pltpu.SMEM((8, 3 * BLOCK), I32),
            dma((9,)),
            dma((48,)),
            dma((12,)),
            dma((2, 2, 2)),
            dma((3, 4)),
            dma((3, 2, 2)),
            dma((3, 4, 2, 2)),
            dma((4,)),
            dma((2, 2)),
            dma((4, 2)),
        ],
        compiler_params=pltpu.CompilerParams(
            collective_id=0, has_side_effects=True, vmem_limit_bytes=67043328
        ),
    )(
        initial.reshape(4, BLOCK, D),
        held_cross,
        weights,
        need_rows.reshape(1, 16),
        tiles[0, 0],
        tile_scale[0],
        tile_src[0],
        tile_dst[0],
        tile_count,
        cross_need.reshape(1, 16),
        cross_tiles[0, 0],
        cross_scale[0],
        cross_src[0],
        cross_dst[0],
    )
    return out[0], out[1]


def solution(mesh):
    in_specs = (
        P(("comm", "dom"), None),
        P(("comm", "dom"), None),
        P(),
        P("comm", "dom", None, None),
        P("comm", "dom", None, None, None),
        P("comm", "dom", None),
        P("comm", "dom", None),
        P("comm", "dom", None),
        P("comm", "dom"),
        P("comm", "dom", None, None),
        P("comm", "dom", None, None, None),
        P("comm", "dom", None),
        P("comm", "dom", None),
        P("comm", "dom", None),
    )
    out_specs = (P(("comm", "dom"), None), P(("comm", "dom"), None))
    return jax.shard_map(
        per_device, mesh=mesh, in_specs=in_specs, out_specs=out_specs, check_vma=False
    )
```

time: 179 us -> 107 us (0.60)
  Pallas kernels: 0 us -> 100 us
  waiting for transfers between devices: 93 us -> 0 us
  matrix products: 26.4 us -> 0 us
  starting transfers between devices: 22 us -> 0 us
  blocking collectives: 15.4 us -> 0 us
  local copies, waits for them, and re-layouts: 18 us -> 5.08 us
    pallas_call x0 -> x1, Pallas kernels: none -> 100 us  [per_device(): pl.pallas_call(kernel, out_shape=(table, table), in_specs=[hbm, hbm, hbm,...]
    all_to_all x5 -> x0, waiting for transfers between devices: 93 us -> none  [the longest x3 68.4 us: fetch(): lax.all_to_all(outgoing, 'dom', split_axis=0, concat_axis=0, tiled=True)]
    dot_general x9 -> x0, matrix products: 26.4 us -> none  [the longest x2 14.4 us: placed(): jnp.einsum('tb,ts,tij->bisj', into, where, tile.astype(jnp.float32), prec...]
    all_to_all x5 -> x0, starting transfers between devices: 22 us -> none  [the longest x3 11.5 us: fetch(): lax.all_to_all(outgoing, 'dom', split_axis=0, concat_axis=0, tiled=True)]
    all_to_all x1 -> x0, blocking collectives: 15.4 us -> none  [per_device(): lax.all_to_all(need_rows, 'dom', split_axis=2, concat_axis=2, tiled=True)]
    gather x4 -> x0, local copies, waits for them, and re-layouts: 9.18 us -> none  [the longest x3 7.15 us: fetch(): outgoing = table[asked].reshape(members, spare, BLOCK, width)]
    unnamed x34 -> x3, local copies, waits for them, and re-layouts: 8.18 us -> 4.49 us
  transfers between devices with their start and end apart: 5 -> 0, of which waited for: 4 -> 0; matrix products, arithmetic and copies ran while one was open for 14% -> 0% of each run, Pallas kernels for 0% -> 0%
where the time goes in v1:
time: 107 us
  Pallas kernels  100 us (93%)
  local copies, waits for them, and re-layouts  5.08 us (5%)
  between operations  1.29 us (1%)
    pallas_call x1, Pallas kernels, per_device(): pl.pallas_call(kernel, out_shape=(table, table), in_specs=[hbm, hbm, hbm,...  100 us
    unnamed x3, local copies, waits for them, and re-layouts  4.49 us

profile of v1, /device:TPU:0, one launch (start us, length us, event | category | flops | bytes accessed | tf_op | source)
XLA Modules:
  0.0 106.9 jit_solution(2646097347378193586)
XLA Ops:
  1.3 0.8 copy.17
  2.0 0.6 reshape.15.xneed_ref
  2.6 100.5 %shard_map.149 = (bf16[512,512]{1,0:T(8,128)(2,1)}, bf16[512,512]{1,0:T(8,128)(2,1)}) custom-call(bf16[4,128,512]{2,1,0:T(8,128)(2,1)} %bitcast.14, bf16[512,512]{1,0:T(8,128)(2,1)} %held_hbm.1, bf16[3,512,512]{2,1,0:T(8,128)(2,1)} %weights_hbm.1, s32[1,16]{1,0:T(1,128)} %bitcast.18, bf16[192,128,128]{2,1,0:T(8,128)(2,1)} %bitcast.12, f32[1,192]{1,0:T(1,128)} %bitcast.15, ...), custom_call_target="tpu_custom_call" | custom-call | tf_op jit(solution)/shard_map/pallas_call | solution.py:484
  103.1 1.9 %copy.21 = bf16[512,512]{1,0:T(8,128)(2,1)} copy(bf16[512,512]{1,0:T(8,128)(2,1)} %get-tuple-element.4) | data formatting | bytes 1048576
  105.0 1.9 %copy.22 = bf16[512,512]{1,0:T(8,128)(2,1)} copy(bf16[512,512]{1,0:T(8,128)(2,1)} %get-tuple-element.5) | data formatting | bytes 1048576

commit v2 on v1

v2 whole, which is shorter than its diff:
```python
import functools
import math

import jax
import jax.numpy as jnp
from jax import lax
from jax.experimental import pallas as pl
from jax.experimental.pallas import tpu as pltpu
from jax.sharding import PartitionSpec as P

BLOCK = 128
D = 512
ROWS = 512
TILES = 192
XTILES = 64
SOURCES = 20
XSOURCES = 16
ALPHA = 0.1
LAMBDA = 0.5
MESH = pl.DeviceIdType.MESH
BF = jnp.bfloat16
F32 = jnp.float32
I32 = jnp.int32
OWN, ANT = 0, 1
CA = 384
CB = D - CA
A = pl.ds(0, CA)
B = pl.ds(CA, CB)


def pair(i):
    return pl.ds(i * 2, 2)


def chain_tables(key_ref, tbl_ref, halves, none, row):
    iota0 = lax.broadcasted_iota(I32, (BLOCK, BLOCK), 0)
    iota1 = lax.broadcasted_iota(I32, (BLOCK, BLOCK), 1)
    last = jnp.full((1, BLOCK), -1, I32)
    prev = [jnp.full((1, BLOCK), -1, I32) for _ in range(halves)]
    for h in range(halves):
        down = jnp.broadcast_to(key_ref[0:1, h * BLOCK : (h + 1) * BLOCK], (BLOCK, BLOCK)).T
        who = iota0 + h * BLOCK
        hit = jnp.where(down == iota1, who, -1)
        last = jnp.maximum(last, jnp.max(hit, axis=0, keepdims=True))
        for j in range(h, halves):
            across = jnp.broadcast_to(key_ref[0:1, j * BLOCK : (j + 1) * BLOCK], (BLOCK, BLOCK))
            same = jnp.logical_and(down == across, who < iota1 + j * BLOCK)
            prev[j] = jnp.maximum(prev[j], jnp.max(jnp.where(same, who, -1), axis=0, keepdims=True))
    tbl_ref[row : row + 1, 0:BLOCK] = jnp.where(last < 0, none, last)
    for j in range(halves):
        tbl_ref[row : row + 1, (j + 1) * BLOCK : (j + 2) * BLOCK] = jnp.where(prev[j] < 0, none, prev[j])


def kernel(
    init_hbm,
    held_hbm,
    weights_hbm,
    need_ref,
    tiles_hbm,
    scale_ref,
    src_ref,
    dst_ref,
    count_ref,
    xneed_ref,
    xtiles_hbm,
    xscale_ref,
    xsrc_ref,
    xdst_ref,
    out_ref,
    ref_ref,
    init,
    held,
    weights,
    tiles,
    slots,
    adj,
    xadj,
    acc,
    xacc,
    rounded,
    hbuf,
    rba,
    rbb,
    anta0,
    anta1,
    anta2,
    xfa,
    zfa,
    agm0,
    agm1,
    agm2,
    agp0,
    agp1,
    agp2,
    agz0,
    agz1,
    agz2,
    xfb,
    nba,
    gba,
    gbb,
    cra,
    crb,
    yfa,
    gxa,
    yagm,
    yagp,
    yagz,
    gxb,
    rq,
    reqs,
    xreqs,
    reqs_s,
    xreqs_s,
    keys,
    tbl,
    tbl_s,
    lsem,
    ssem,
    qsem,
    xsa,
    asa,
    zsa,
    rsa,
    ags,
    xsb,
    rsb,
    rpb,
    ns,
    yss,
    csa,
    yags,
    csb,
):
    comm = lax.axis_index("comm")
    dom = lax.axis_index("dom")
    y, xl = comm // 2, comm % 2
    z, xh, c = dom // 4, (dom // 2) % 2, dom % 2
    x = xh * 2 + xl

    def dev(px, py, pz, pc):
        return (py * 2 + px % 2, pz * 4 + (px // 2) * 2 + pc)

    xp, xm, x2 = (x + 1) % 4, (x + 3) % 4, (x + 2) % 4
    xnb = xh * 2 + (1 - xl)
    xot = (x + 3 + 2 * xl) % 4
    zp, zm, z2 = (z + 1) % 4, (z + 3) % 4, (z + 2) % 4
    yp, ym, y2 = (y + 1) % 4, (y + 3) % 4, (y + 2) % 4
    rel_z = (z, zm, zp, z2)
    rel_y = (y, ym, yp, y2)
    anta = (anta0, anta1, anta2)
    agm, agp, agz = (agm0, agm1, agm2), (agp0, agp1, agp2), (agz0, agz1, agz2)
    partner = dev(x, y, z, 1 - c)

    loads = {}

    def load(name, src, dst, i):
        loads[name] = pltpu.make_async_copy(src, dst, lsem.at[i])
        loads[name].start()

    load("init", init_hbm, init, 0)
    load("tiles0", tiles_hbm.at[pl.ds(0, 96)], tiles.at[pl.ds(0, 96)], 1)
    load("tiles1", tiles_hbm.at[pl.ds(96, 96)], tiles.at[pl.ds(96, 96)], 2)
    load("held", held_hbm, held, 3)
    load("weights", weights_hbm, weights, 4)

    barrier = pltpu.get_barrier_semaphore()
    column = [dev(x, y, pz, pc) for pz in (zp, zm, z2) for pc in range(2)]
    across = [dev(x2, y, z, pc) for pc in range(2)]
    peers = [dev(xp, y, z, 0), dev(xp, y, z, 1), dev(xm, y, z, 0), dev(xm, y, z, 1), partner] + column + across
    peers += [dev(x, py, z, c) for py in (yp, ym, y2)]
    for peer in peers:
        pl.semaphore_signal(barrier, inc=1, device_id=peer, device_id_type=MESH)
    rq[0:1, 0:16] = need_ref[...]
    rq[1:3, 0:8] = xneed_ref[...]
    loads["init"].wait()
    pl.semaphore_wait(barrier, len(peers))

    sent = []

    def send(src, dst, sem, device):
        copy = pltpu.make_async_remote_copy(
            src_ref=src,
            dst_ref=dst,
            send_sem=ssem.at[len(sent)],
            recv_sem=sem,
            device_id=device,
            device_id_type=MESH,
        )
        copy.start()
        sent.append(copy)

    def arrived(dst, sem):
        pltpu.make_async_remote_copy(
            src_ref=dst,
            dst_ref=dst,
            send_sem=ssem.at[0],
            recv_sem=sem,
            device_id=partner,
            device_id_type=MESH,
        ).wait_recv()

    def drain():
        for copy in sent:
            copy.wait_send()
        sent.clear()

    def part(pz, ty, pc):
        return pz * 4 + (xh if ty == OWN else 1 - xh) * 2 + pc

    def group(py, ty):
        return py * 2 + (xl if ty == OWN else 1 - xl)


    def xa_first(e, table, half):
        device = dev(xp, y, z, c) if half == 0 else dev(xm, y, z, c)
        for k in range(2):
            send(table.at[2 * half + k, :, A], xfa.at[e, half, k], xsa.at[e, half, k], device)

    def xa_forward(e, k):
        for half in range(2):
            arrived(xfa.at[e, half, k], xsa.at[e, half, k])
            device = dev(xp, y, z, c) if half == 0 else dev(xm, y, z, c)
            send(xfa.at[e, half, k], anta[e].at[2 * half + k], asa.at[e, 2 * half + k], device)

    def xa_done(e):
        for k in range(4):
            arrived(anta[e].at[k], asa.at[e, k])

    def za_gather(ty, table, g, pz, pc, p):
        want = reqs_s[pz * 2 + pc, 0, p]
        gba[ty, g] = table[want, :, A]
        return gba.at[ty, g]

    def za_first(e, ty, table):
        p = part(z, ty, c)
        send(za_gather(ty, table, 0, z2, 0, p), zfa.at[e, 0, ty], zsa.at[e, 0, ty], dev(x, y, zp, c))
        send(za_gather(ty, table, 1, z2, 1, p), zfa.at[e, 1, ty], zsa.at[e, 1, ty], dev(x, y, zm, c))

    def za_rest(e, ty, table):
        p = part(z, ty, c)
        mine = rba.at[e, p]
        send(za_gather(ty, table, 2, zp, 0, p), mine, rsa.at[e, 0, ty, c], dev(x, y, zp, 0))
        send(za_gather(ty, table, 3, zm, 0, p), mine, rsa.at[e, 1, ty, c], dev(x, y, zm, 0))
        send(za_gather(ty, table, 4, zp, 1, p), mine, rsa.at[e, 0, ty, c], dev(x, y, zp, 1))
        send(za_gather(ty, table, 5, zm, 1, p), mine, rsa.at[e, 1, ty, c], dev(x, y, zm, 1))
        send(za_gather(ty, table, 6, z, 1 - c, p), mine, rsa.at[e, 3, ty, 0], partner)
        want = reqs_s[z * 2 + c, 0, p]
        rba[e, p] = table[want, :, A]

    def za_forward(e, ty):
        arrived(zfa.at[e, 0, ty], zsa.at[e, 0, ty])
        send(zfa.at[e, 0, ty], rba.at[e, part(zm, ty, c)], rsa.at[e, 2, ty, c], dev(x, y, zp, 0))
        arrived(zfa.at[e, 1, ty], zsa.at[e, 1, ty])
        send(zfa.at[e, 1, ty], rba.at[e, part(zp, ty, c)], rsa.at[e, 2, ty, c], dev(x, y, zm, 1))


    def ring_first(table, fromm, fromp, sems, up, down):
        low, high = pl.ds(0, 2), pl.ds(2, 2)
        send(table.at[low, :, B], fromm.at[low], sems[0, 0], up)
        send(table.at[high, :, B], fromp.at[high], sems[1, 0], down)
        send(table.at[high, :, B], fromm.at[high], sems[0, 1], up)
        send(table.at[low, :, B], fromp.at[low], sems[1, 1], down)

    def ring_forward(fromm, fromp, far, sems, up, down):
        low, high = pl.ds(0, 2), pl.ds(2, 2)
        arrived(fromm.at[low], sems[0, 0])
        send(fromm.at[low], far.at[low], sems[2, 0], up)
        arrived(fromp.at[high], sems[1, 0])
        send(fromp.at[high], far.at[high], sems[2, 1], down)

    def ring_done(fromm, fromp, sems):
        arrived(fromm.at[pl.ds(2, 2)], sems[0, 1])
        arrived(fromp.at[pl.ds(0, 2)], sems[1, 1])

    def ring_far_done(far, sems):
        arrived(far.at[pl.ds(0, 2)], sems[2, 0])
        arrived(far.at[pl.ds(2, 2)], sems[2, 1])

    def zring(e):
        sems = {(i, j): ags.at[e, i, j] for i in range(3) for j in range(2)}
        return agm[e], agp[e], agz[e], sems, dev(x, y, zp, c), dev(x, y, zm, c)

    def zb_first(e, table):
        m, p, _, sems, up, down = zring(e)
        ring_first(table, m, p, sems, up, down)

    def zb_forward(e):
        ring_forward(*zring(e))

    def zb_done(e):
        m, p, _, sems, _, _ = zring(e)
        ring_done(m, p, sems)

    def zb_far_done(e):
        _, _, far, sems, _, _ = zring(e)
        ring_far_done(far, sems)

    def xb_first(e, r, own=None):
        table = (own, agm[e], agp[e], agz[e])[r]
        p = part(rel_z[r], OWN, c)

        def wanted(row):
            want = reqs_s[row, 0, p]
            return table[want, :, B] if r == 0 else table[want]

        gbb[3 * r] = wanted(8)
        send(gbb.at[3 * r], xfb.at[e, 0, r], xsb.at[e, 0, r], dev(xp, y, z, c))
        gbb[3 * r + 1] = wanted(9)
        send(gbb.at[3 * r + 1], xfb.at[e, 1, r], xsb.at[e, 1, r], dev(xm, y, z, c))
        gbb[3 * r + 2] = wanted(z * 2 + 1 - c)
        send(gbb.at[3 * r + 2], rbb.at[e, p], rpb.at[e, r], partner)
        rbb[e, p] = wanted(z * 2 + c)

    def xb_forward(e, r):
        arrived(xfb.at[e, 0, r], xsb.at[e, 0, r])
        send(xfb.at[e, 0, r], rbb.at[e, rel_z[r] * 4 + (xm // 2) * 2 + c], rsb.at[e, r, c], dev(xp, y, z, 0))
        arrived(xfb.at[e, 1, r], xsb.at[e, 1, r])
        send(xfb.at[e, 1, r], rbb.at[e, rel_z[r] * 4 + (xp // 2) * 2 + c], rsb.at[e, r, c], dev(xm, y, z, 1))


    def dot_into(total, lhs, rhs, start, width, first=False):
        for n in range(0, width, 256):
            w = min(256, width - n)
            cols = pl.ds(start + n, w)
            value = jnp.dot(lhs[...], rhs[:, :, n : n + w].reshape(256, w), preferred_element_type=F32)
            if first:
                total[:, cols] = value
            else:
                total[:, cols] += value

    def dot_own(table):
        dot_into(acc, adj.at[0], table.at[pl.ds(0, 2)], 0, D, first=True)
        dot_into(acc, adj.at[1], table.at[pl.ds(2, 2)], 0, D)

    def dot_a(e, ty, key):
        pz = (zm, zp, z2, z)[key]
        if key == 3:
            arrived(rba.at[e, part(z, ty, 1 - c)], rsa.at[e, 3, ty, 0])
        else:
            for pc in range(2):
                arrived(rba.at[e, part(pz, ty, pc)], rsa.at[e, key, ty, pc])
        j = pz * 2 + (xh if ty == OWN else 1 - xh)
        dot_into(acc, adj.at[2 + j], rba.at[e, pair(j)], 0, CA)

    def dot_b(e, ty, r):
        if ty == OWN:
            arrived(rbb.at[e, part(rel_z[r], OWN, 1 - c)], rpb.at[e, r])
        else:
            for pc in range(2):
                arrived(rbb.at[e, part(rel_z[r], ANT, pc)], rsb.at[e, r, pc])
        j = rel_z[r] * 2 + (xh if ty == OWN else 1 - xh)
        dot_into(acc, adj.at[2 + j], rbb.at[e, pair(j)], CA, CB)

    def layer(level, added, target, after=lambda half: None, blocks=True):
        beta = math.log(LAMBDA / level + 1.0)
        for half in range(2):
            rows = pl.ds(half * 256, 256)
            total = acc[rows, :] + added[rows, :].astype(F32)
            mixed = (1.0 - ALPHA) * total + ALPHA * init[2 * half : 2 * half + 2].reshape(256, D).astype(F32)
            acc[rows, :] = mixed
            rounded[rows, :] = mixed.astype(BF)
            for n in range(2):
                cols = pl.ds(n * 256, 256)
                turned = jnp.dot(rounded[rows, :], weights[level - 1, :, cols], preferred_element_type=F32)
                done = jax.nn.relu((1.0 - beta) * acc[rows, cols] + beta * turned).astype(BF)
                if blocks:
                    target[2 * half : 2 * half + 2, :, cols] = done.reshape(2, BLOCK, 256)
                else:
                    target[rows, cols] = done
            after(half)


    def chain(tile_ref, scales, row, start, stop):
        @pl.loop(start, stop)
        def _(t):
            before = tbl_s[row, BLOCK + t]
            slots[t] = slots[before] + scales[0, t] * tile_ref[t].astype(F32)

    def place(target, row, sources):
        @pl.loop(0, sources // 2)
        def _(s2):
            for b in range(4):
                for s in range(2):
                    final = tbl_s[row, b * sources + s2 * 2 + s]
                    target[s2, b * BLOCK : (b + 1) * BLOCK, s * BLOCK : (s + 1) * BLOCK] = slots[final].astype(BF)

    for device in column + [partner]:
        send(rq, reqs.at[z * 2 + c], qsem.at[z * 2 + c], device)
    for device in across:
        send(rq, reqs.at[8 + c], qsem.at[8 + c], device)
    for py in (yp, ym, y2):
        send(rq, xreqs.at[y], qsem.at[10 + y], dev(x, py, z, c))
    send(rq, xreqs.at[4], qsem.at[14], dev(xnb, y, z, c))
    xa_first(0, init, 0)
    xa_first(0, init, 1)
    zb_first(0, init)
    reqs[z * 2 + c] = rq[...]
    xreqs[y] = rq[...]

    keys[...] = jnp.full((8, 256), -1, I32)
    live = count_ref[0, 0]
    at = lax.broadcasted_iota(I32, (1, TILES), 1)
    keys[0:1, 0:TILES] = jnp.where(at < live, dst_ref[...] * SOURCES + src_ref[...], -1)
    chain_tables(keys, tbl, 2, TILES, 0)
    keys[0:1, 0:256] = jnp.full((1, 256), -1, I32)
    keys[0:1, 0:XTILES] = xdst_ref[...] * XSOURCES + xsrc_ref[...]
    chain_tables(keys, tbl, 1, TILES, 1)
    copy_tbl = pltpu.make_async_copy(tbl, tbl_s, lsem.at[5])
    copy_tbl.start()
    slots[TILES] = jnp.zeros((BLOCK, BLOCK), F32)

    for pz in (zp, zm, z2):
        for pc in range(2):
            arrived(reqs.at[pz * 2 + pc], qsem.at[pz * 2 + pc])
    arrived(reqs.at[z * 2 + 1 - c], qsem.at[z * 2 + 1 - c])
    for pc in range(2):
        arrived(reqs.at[8 + pc], qsem.at[8 + pc])
    copy_req = pltpu.make_async_copy(reqs, reqs_s, lsem.at[6])
    copy_req.start()
    copy_req.wait()

    def begin(e, table):
        za_first(e, OWN, table)
        xb_first(e, 0, table)

    begin(0, init)
    zb_forward(0)
    za_rest(0, OWN, init)
    for py in (yp, ym, y2):
        arrived(xreqs.at[py], qsem.at[10 + py])
    arrived(xreqs.at[4], qsem.at[14])
    copy_xreq = pltpu.make_async_copy(xreqs, xreqs_s, lsem.at[7])
    copy_xreq.start()
    copy_xreq.wait()
    copy_tbl.wait()
    loads["tiles0"].wait()
    xa_forward(0, 0)
    zb_done(0)
    xb_first(0, 1)
    xb_first(0, 2)
    chain(tiles, scale_ref, 0, 0, 32)
    xa_forward(0, 1)
    chain(tiles, scale_ref, 0, 32, 64)
    za_forward(0, OWN)
    xb_forward(0, 0)
    zb_far_done(0)
    xb_first(0, 3)
    chain(tiles, scale_ref, 0, 64, 96)
    loads["tiles1"].wait()
    xb_forward(0, 1)
    xb_forward(0, 2)
    chain(tiles, scale_ref, 0, 96, 144)
    xa_done(0)
    za_first(0, ANT, anta[0])
    za_rest(0, ANT, anta[0])
    xb_forward(0, 3)
    chain(tiles, scale_ref, 0, 144, 192)
    load("xtiles", xtiles_hbm, tiles.at[pl.ds(0, XTILES)], 8)
    place(adj, 0, SOURCES)
    dot_own(init)
    za_forward(0, ANT)
    for key in (3, 0, 1, 2):
        dot_a(0, OWN, key)
    for r in range(4):
        dot_b(0, OWN, r)
        dot_b(0, ANT, r)
    loads["held"].wait()
    loads["weights"].wait()
    for key in (3, 0, 1, 2):
        dot_a(0, ANT, key)
    drain()
    layer(1, held, hbuf.at[0], lambda half: xa_first(1, hbuf.at[0], half))

    h1 = hbuf.at[0]
    zb_first(1, h1)
    begin(1, h1)
    dot_own(h1)
    zb_forward(1)
    za_rest(1, OWN, h1)
    xa_forward(1, 0)
    zb_done(1)
    xb_first(1, 1)
    xb_first(1, 2)
    dot_a(1, OWN, 3)
    dot_b(1, OWN, 0)
    xa_forward(1, 1)
    xb_forward(1, 0)
    za_forward(1, OWN)
    zb_far_done(1)
    xb_first(1, 3)
    dot_b(1, OWN, 1)
    dot_b(1, OWN, 2)
    dot_b(1, OWN, 3)
    xb_forward(1, 1)
    xb_forward(1, 2)
    xa_done(1)
    za_first(1, ANT, anta[1])
    za_rest(1, ANT, anta[1])
    xb_forward(1, 3)
    dot_a(1, OWN, 0)
    dot_a(1, OWN, 1)
    dot_a(1, OWN, 2)
    dot_a(1, ANT, 3)
    dot_b(1, ANT, 0)
    za_forward(1, ANT)
    loads["xtiles"].wait()
    chain(tiles, xscale_ref, 1, 0, XTILES)
    place(xadj, 1, XSOURCES)
    for r in range(1, 4):
        dot_b(1, ANT, r)
    for key in (0, 1, 2):
        dot_a(1, ANT, key)
    drain()

    h2 = hbuf.at[1]

    def na_first(half):
        for k in range(2 * half, 2 * half + 2):
            send(h2.at[k, :, A], nba.at[k], ns.at[k], dev(xnb, y, z, c))

    def na_forward(k):
        arrived(nba.at[k], ns.at[k])
        send(nba.at[k], anta[2].at[k], asa.at[2, k], dev(xot, y, z, c))

    def ya_gather(ty, table, g, py, k):
        want = xreqs_s[py, 1 + k, group(y, ty)]
        gxa[ty, g] = table[want, :, A]

    def ya_first(ty, table):
        ya_gather(ty, table, 0, y2, 0)
        send(gxa.at[ty, 0], yfa.at[0, ty], yss.at[0, ty], dev(x, yp, z, c))
        ya_gather(ty, table, 1, y2, 1)
        send(gxa.at[ty, 1], yfa.at[1, ty], yss.at[1, ty], dev(x, ym, z, c))

    def ya_rest(ty, table):
        mine = cra.at[pair(group(y, ty))]
        for i, py in enumerate((yp, ym)):
            ya_gather(ty, table, 2 + 2 * i, py, 0)
            ya_gather(ty, table, 3 + 2 * i, py, 1)
            send(gxa.at[ty, pair(1 + i)], mine, csa.at[i, ty], dev(x, py, z, c))
        for k in range(2):
            want = xreqs_s[y, 1 + k, group(y, ty)]
            cra[group(y, ty) * 2 + k] = table[want, :, A]

    def ya_forward(ty):
        arrived(yfa.at[0, ty], yss.at[0, ty])
        send(yfa.at[0, ty], cra.at[group(ym, ty) * 2], csa.at[2, ty], dev(x, yp, z, c))
        arrived(yfa.at[1, ty], yss.at[1, ty])
        send(yfa.at[1, ty], cra.at[group(yp, ty) * 2 + 1], csa.at[3, ty], dev(x, ym, z, c))

    ysems = {(i, j): yags.at[i, j] for i in range(3) for j in range(2)}
    yring = (yagm, yagp, yagz, ysems, dev(x, yp, z, c), dev(x, ym, z, c))

    def yb_first(r):
        table = (h2, yagm, yagp, yagz)[r]
        g = group(rel_y[r], OWN)
        for k in range(2):
            for row, keep in ((4, False), (y, True)):
                want = xreqs_s[row, 1 + k, g]
                value = table[want, :, B] if r == 0 else table[want]
                if keep:
                    crb[g * 2 + k] = value
                else:
                    gxb[2 * r + k] = value
        send(gxb.at[pl.ds(2 * r, 2)], crb.at[pair(g)], csb.at[r], dev(xnb, y, z, c))

    def cross_a(ty, key, first=False):
        py = (ym, yp, y2, y)[key]
        g = group(py, ty)
        if key < 2:
            arrived(cra.at[pair(g)], csa.at[key, ty])
        if key == 2:
            arrived(cra.at[g * 2], csa.at[2, ty])
            arrived(cra.at[g * 2 + 1], csa.at[3, ty])
        dot_into(xacc, xadj.at[g], cra.at[pair(g)], 0, CA, first)

    def cross_b(ty, r, first=False):
        g = group(rel_y[r], ty)
        if ty == ANT:
            arrived(crb.at[pair(g)], csb.at[r])
        dot_into(xacc, xadj.at[g], crb.at[pair(g)], CA, CB, first)

    layer(2, held, h2, na_first)
    zb_first(2, h2)
    ring_first(h2, yagm, yagp, ysems, dev(x, yp, z, c), dev(x, ym, z, c))
    za_first(2, OWN, h2)
    ya_first(OWN, h2)
    xb_first(2, 0, h2)
    zb_forward(2)
    ring_forward(*yring)
    za_rest(2, OWN, h2)
    ya_rest(OWN, h2)
    na_forward(0)
    zb_done(2)
    xb_first(2, 1)
    xb_first(2, 2)
    yb_first(0)
    na_forward(1)
    ring_done(yagm, yagp, ysems)
    yb_first(1)
    yb_first(2)
    dot_own(h2)
    na_forward(2)
    za_forward(2, OWN)
    ya_forward(OWN)
    zb_far_done(2)
    xb_first(2, 3)
    ring_far_done(yagz, ysems)
    yb_first(3)
    na_forward(3)
    ya_first(ANT, nba)
    ya_rest(ANT, nba)
    xb_forward(2, 0)
    cross_a(OWN, 3, first=True)
    cross_a(ANT, 3)
    cross_b(OWN, 0, first=True)
    xb_forward(2, 1)
    xb_forward(2, 2)
    xa_done(2)
    za_first(2, ANT, anta[2])
    za_rest(2, ANT, anta[2])
    xb_forward(2, 3)
    for key in (3, 0, 1):
        dot_a(2, OWN, key)
    cross_a(OWN, 0)
    cross_a(OWN, 1)
    ya_forward(ANT)
    za_forward(2, ANT)
    for r in range(1, 4):
        cross_b(OWN, r)
    dot_a(2, OWN, 2)
    cross_a(OWN, 2)
    for r in range(4):
        dot_b(2, OWN, r)
    dot_a(2, ANT, 3)
    for r in range(4):
        dot_b(2, ANT, r)
        cross_b(ANT, r)
    cross_a(ANT, 0)
    cross_a(ANT, 1)
    dot_a(2, ANT, 0)
    dot_a(2, ANT, 1)
    cross_a(ANT, 2)
    ref_ref[...] = xacc[...].astype(BF)
    dot_a(2, ANT, 2)
    layer(3, ref_ref, out_ref, blocks=False)
    drain()


def per_device(
    initial,
    held_cross,
    weights,
    need_rows,
    tiles,
    tile_scale,
    tile_src,
    tile_dst,
    tile_count,
    cross_need,
    cross_tiles,
    cross_scale,
    cross_src,
    cross_dst,
):
    hbm = pl.BlockSpec(memory_space=pl.ANY)
    vmem = pl.BlockSpec(memory_space=pltpu.VMEM)
    smem = pl.BlockSpec(memory_space=pltpu.SMEM)
    dma = pltpu.SemaphoreType.DMA
    table = jax.ShapeDtypeStruct((ROWS, D), BF)
    out = pl.pallas_call(
        kernel,
        out_shape=(table, table),
        in_specs=[hbm, hbm, hbm, vmem, hbm, smem, vmem, vmem, smem, vmem, hbm, smem, vmem, vmem],
        out_specs=(vmem, vmem),
        scratch_shapes=[
            pltpu.VMEM((4, BLOCK, D), BF),
            pltpu.VMEM((ROWS, D), BF),
            pltpu.VMEM((3, D, D), BF),
            pltpu.VMEM((TILES, BLOCK, BLOCK), BF),
            pltpu.VMEM((TILES + 1, BLOCK, BLOCK), F32),
            pltpu.VMEM((SOURCES // 2, ROWS, 2 * BLOCK), BF),
            pltpu.VMEM((XSOURCES // 2, ROWS, 2 * BLOCK), BF),
            pltpu.VMEM((ROWS, D), F32),
            pltpu.VMEM((ROWS, D), F32),
            pltpu.VMEM((ROWS, D), BF),
            pltpu.VMEM((2, 4, BLOCK, D), BF),
            pltpu.VMEM((3, 16, BLOCK, CA), BF),
            pltpu.VMEM((3, 16, BLOCK, CB), BF),
            pltpu.VMEM((4, BLOCK, CA), BF),
            pltpu.VMEM((4, BLOCK, CA), BF),
            pltpu.VMEM((4, BLOCK, CA), BF),
            pltpu.VMEM((2, 2, 2, BLOCK, CA), BF),
            pltpu.VMEM((3, 2, 2, BLOCK, CA), BF),
            pltpu.VMEM((4, BLOCK, CB), BF),
            pltpu.VMEM((4, BLOCK, CB), BF),
            pltpu.VMEM((4, BLOCK, CB), BF),
            pltpu.VMEM((4, BLOCK, CB), BF),
            pltpu.VMEM((4, BLOCK, CB), BF),
            pltpu.VMEM((4, BLOCK, CB), BF),
            pltpu.VMEM((4, BLOCK, CB), BF),
            pltpu.VMEM((4, BLOCK, CB), BF),
            pltpu.VMEM((4, BLOCK, CB), BF),
            pltpu.VMEM((3, 2, 4, BLOCK, CB), BF),
            pltpu.VMEM((4, BLOCK, CA), BF),
            pltpu.VMEM((2, 7, BLOCK, CA), BF),
            pltpu.VMEM((12, BLOCK, CB), BF),
            pltpu.VMEM((16, BLOCK, CA), BF),
            pltpu.VMEM((16, BLOCK, CB), BF),
            pltpu.VMEM((2, 2, BLOCK, CA), BF),
            pltpu.VMEM((2, 6, BLOCK, CA), BF),
            pltpu.VMEM((4, BLOCK, CB), BF),
            pltpu.VMEM((4, BLOCK, CB), BF),
            pltpu.VMEM((4, BLOCK, CB), BF),
            pltpu.VMEM((8, BLOCK, CB), BF),
            pltpu.VMEM((4, BLOCK), I32),
            pltpu.VMEM((10, 4, BLOCK), I32),
            pltpu.VMEM((5, 4, BLOCK), I32),
            pltpu.SMEM((10, 4, BLOCK), I32),
            pltpu.SMEM((5, 4, BLOCK), I32),
            pltpu.VMEM((8, 2 * BLOCK), I32),
            pltpu.VMEM((8, 3 * BLOCK), I32),
            pltpu.SMEM((8, 3 * BLOCK), I32),
            dma((9,)),
            dma((96,)),
            dma((15,)),
            dma((2, 2, 2)),
            dma((3, 4)),
            dma((3, 2, 2)),
            dma((3, 4, 2, 2)),
            dma((3, 3, 2)),
            dma((3, 2, 4)),
            dma((3, 4, 2)),
            dma((3, 4)),
            dma((4,)),
            dma((2, 2)),
            dma((4, 2)),
            dma((3, 2)),
            dma((4,)),
        ],
        compiler_params=pltpu.CompilerParams(
            collective_id=0, has_side_effects=True, vmem_limit_bytes=67043328
        ),
    )(
        initial.reshape(4, BLOCK, D),
        held_cross,
        weights,
        need_rows.reshape(1, 16),
        tiles[0, 0],
        tile_scale[0],
        tile_src[0],
        tile_dst[0],
        tile_count,
        cross_need[0, 0].T,
        cross_tiles[0, 0],
        cross_scale[0],
        cross_src[0],
        cross_dst[0],
    )
    return out[0], out[1]


def solution(mesh):
    in_specs = (
        P(("comm", "dom"), None),
        P(("comm", "dom"), None),
        P(),
        P("comm", "dom", None, None),
        P("comm", "dom", None, None, None),
        P("comm", "dom", None),
        P("comm", "dom", None),
        P("comm", "dom", None),
        P("comm", "dom"),
        P("comm", "dom", None, None),
        P("comm", "dom", None, None, None),
        P("comm", "dom", None),
        P("comm", "dom", None),
        P("comm", "dom", None),
    )
    out_specs = (P(("comm", "dom"), None), P(("comm", "dom"), None))
    return jax.shard_map(
        per_device, mesh=mesh, in_specs=in_specs, out_specs=out_specs, check_vma=False
    )
```

time: 107 us -> 96 us (0.90)
  Pallas kernels: 100 us -> 90.8 us
  local copies, waits for them, and re-layouts: 5.08 us -> 3.74 us
    pallas_call x1, Pallas kernels: 100 us -> 90.8 us  [per_device(): pl.pallas_call(kernel, out_shape=(table, table), in_specs=[hbm, hbm, hbm,...]
    unnamed x3 -> x2, local copies, waits for them, and re-layouts: 4.49 us -> 3.74 us
where the time goes in v2:
time: 96 us; the launch traced here: 95.8 us
  Pallas kernels  90.8 us (95%)
  local copies, waits for them, and re-layouts  3.74 us (4%)
  between operations  1.29 us (1%)
    pallas_call x1, Pallas kernels, per_device(): pl.pallas_call(kernel, out_shape=(table, table), in_specs=[hbm, hbm, hbm,...  90.8 us
    unnamed x2, local copies, waits for them, and re-layouts  3.74 us

profile of v2, /device:TPU:0, one launch (start us, length us, event | category | flops | bytes accessed | tf_op | source)
XLA Modules:
  0.0 95.8 jit_solution(2709446251499545622)
XLA Ops:
  1.3 90.8 %shard_map.149 = (bf16[512,512]{1,0:T(8,128)(2,1)}, bf16[512,512]{1,0:T(8,128)(2,1)}) custom-call(bf16[4,128,512]{2,1,0:T(8,128)(2,1)} %bitcast.15, bf16[512,512]{1,0:T(8,128)(2,1)} %held_hbm.1, bf16[3,512,512]{2,1,0:T(8,128)(2,1)} %weights_hbm.1, s32[1,16]{1,0:T(1,128)} %bitcast.20, bf16[192,128,128]{2,1,0:T(8,128)(2,1)} %bitcast.13, f32[1,192]{1,0:T(1,128)} %bitcast.16, ...), custom_call_target="tpu_custom_call" | custom-call | tf_op jit(solution)/shard_map/pallas_call | solution.py:672
  92.0 1.9 %copy.19 = bf16[512,512]{1,0:T(8,128)(2,1)} copy(bf16[512,512]{1,0:T(8,128)(2,1)} %get-tuple-element.4) | data formatting | bytes 1048576
  93.9 1.9 %copy.20 = bf16[512,512]{1,0:T(8,128)(2,1)} copy(bf16[512,512]{1,0:T(8,128)(2,1)} %get-tuple-element.5) | data formatting | bytes 1048576

commit v3 on v2

--- a/solution.py
+++ b/solution.py
@@ -22,10 +22,8 @@
 F32 = jnp.float32
 I32 = jnp.int32
 OWN, ANT = 0, 1
-CA = 384
-CB = D - CA
-A = pl.ds(0, CA)
-B = pl.ds(CA, CB)
+CA = (256, 256, 384)
+CB = tuple(D - n for n in CA)
 
 
 def pair(i):
@@ -79,13 +77,19 @@
     xacc,
     rounded,
     hbuf,
-    rba,
-    rbb,
+    rba0,
+    rba1,
+    rba2,
+    rbb0,
+    rbb1,
+    rbb2,
     anta0,
     anta1,
     anta2,
     xfa,
-    zfa,
+    zfa0,
+    zfa1,
+    zfa2,
     agm0,
     agm1,
     agm2,
@@ -95,10 +99,15 @@
     agz0,
     agz1,
     agz2,
-    xfb,
+    xfb0,
+    xfb1,
+    xfb2,
     nba,
-    gba,
-    gbb,
+    xfo,
+    gba0,
+    gba2,
+    gbb0,
+    gbb2,
     cra,
     crb,
     yfa,
@@ -127,6 +136,7 @@
     rsb,
     rpb,
     ns,
+    os,
     yss,
     csa,
     yags,
@@ -151,6 +161,12 @@
     anta = (anta0, anta1, anta2)
     agm, agp, agz = (agm0, agm1, agm2), (agp0, agp1, agp2), (agz0, agz1, agz2)
     partner = dev(x, y, z, 1 - c)
+
+    rba, rbb = (rba0, rba1, rba2), (rbb0, rbb1, rbb2)
+    zfa, xfb = (zfa0, zfa1, zfa2), (xfb0, xfb1, xfb2)
+    gba, gbb = (gba0, gba0, gba2), (gbb0, gbb0, gbb2)
+    cols_a = tuple(pl.ds(0, n) for n in CA)
+    cols_b = tuple(pl.ds(n, D - n) for n in CA)
 
     loads = {}
 
@@ -215,7 +231,7 @@
     def xa_first(e, table, half):
         device = dev(xp, y, z, c) if half == 0 else dev(xm, y, z, c)
         for k in range(2):
-            send(table.at[2 * half + k, :, A], xfa.at[e, half, k], xsa.at[e, half, k], device)
+            send(table.at[2 * half + k, :, cols_a[e]], xfa.at[e, half, k], xsa.at[e, half, k], device)
 
     def xa_forward(e, k):
         for half in range(2):
@@ -227,40 +243,40 @@
         for k in range(4):
             arrived(anta[e].at[k], asa.at[e, k])
 
-    def za_gather(ty, table, g, pz, pc, p):
+    def za_gather(e, ty, table, g, pz, pc, p):
         want = reqs_s[pz * 2 + pc, 0, p]
-        gba[ty, g] = table[want, :, A]
-        return gba.at[ty, g]
+        gba[e][ty, g] = table[want, :, cols_a[e]]
+        return gba[e].at[ty, g]
 
     def za_first(e, ty, table):
         p = part(z, ty, c)
-        send(za_gather(ty, table, 0, z2, 0, p), zfa.at[e, 0, ty], zsa.at[e, 0, ty], dev(x, y, zp, c))
-        send(za_gather(ty, table, 1, z2, 1, p), zfa.at[e, 1, ty], zsa.at[e, 1, ty], dev(x, y, zm, c))
+        send(za_gather(e, ty, table, 0, z2, 0, p), zfa[e].at[0, ty], zsa.at[e, 0, ty], dev(x, y, zp, c))
+        send(za_gather(e, ty, table, 1, z2, 1, p), zfa[e].at[1, ty], zsa.at[e, 1, ty], dev(x, y, zm, c))
 
     def za_rest(e, ty, table):
         p = part(z, ty, c)
-        mine = rba.at[e, p]
-        send(za_gather(ty, table, 2, zp, 0, p), mine, rsa.at[e, 0, ty, c], dev(x, y, zp, 0))
-        send(za_gather(ty, table, 3, zm, 0, p), mine, rsa.at[e, 1, ty, c], dev(x, y, zm, 0))
-        send(za_gather(ty, table, 4, zp, 1, p), mine, rsa.at[e, 0, ty, c], dev(x, y, zp, 1))
-        send(za_gather(ty, table, 5, zm, 1, p), mine, rsa.at[e, 1, ty, c], dev(x, y, zm, 1))
-        send(za_gather(ty, table, 6, z, 1 - c, p), mine, rsa.at[e, 3, ty, 0], partner)
+        mine = rba[e].at[p]
+        send(za_gather(e, ty, table, 2, zp, 0, p), mine, rsa.at[e, 0, ty, c], dev(x, y, zp, 0))
+        send(za_gather(e, ty, table, 3, zm, 0, p), mine, rsa.at[e, 1, ty, c], dev(x, y, zm, 0))
+        send(za_gather(e, ty, table, 4, zp, 1, p), mine, rsa.at[e, 0, ty, c], dev(x, y, zp, 1))
+        send(za_gather(e, ty, table, 5, zm, 1, p), mine, rsa.at[e, 1, ty, c], dev(x, y, zm, 1))
+        send(za_gather(e, ty, table, 6, z, 1 - c, p), mine, rsa.at[e, 3, ty, 0], partner)
         want = reqs_s[z * 2 + c, 0, p]
-        rba[e, p] = table[want, :, A]
+        rba[e][p] = table[want, :, cols_a[e]]
 
     def za_forward(e, ty):
-        arrived(zfa.at[e, 0, ty], zsa.at[e, 0, ty])
-        send(zfa.at[e, 0, ty], rba.at[e, part(zm, ty, c)], rsa.at[e, 2, ty, c], dev(x, y, zp, 0))
-        arrived(zfa.at[e, 1, ty], zsa.at[e, 1, ty])
-        send(zfa.at[e, 1, ty], rba.at[e, part(zp, ty, c)], rsa.at[e, 2, ty, c], dev(x, y, zm, 1))
-
-
-    def ring_first(table, fromm, fromp, sems, up, down):
+        arrived(zfa[e].at[0, ty], zsa.at[e, 0, ty])
+        send(zfa[e].at[0, ty], rba[e].at[part(zm, ty, c)], rsa.at[e, 2, ty, c], dev(x, y, zp, 0))
+        arrived(zfa[e].at[1, ty], zsa.at[e, 1, ty])
+        send(zfa[e].at[1, ty], rba[e].at[part(zp, ty, c)], rsa.at[e, 2, ty, c], dev(x, y, zm, 1))
+
+
+    def ring_first(table, b, fromm, fromp, sems, up, down):
         low, high = pl.ds(0, 2), pl.ds(2, 2)
-        send(table.at[low, :, B], fromm.at[low], sems[0, 0], up)
-        send(table.at[high, :, B], fromp.at[high], sems[1, 0], down)
-        send(table.at[high, :, B], fromm.at[high], sems[0, 1], up)
-        send(table.at[low, :, B], fromp.at[low], sems[1, 1], down)
+        send(table.at[low, :, b], fromm.at[low], sems[0, 0], up)
+        send(table.at[high, :, b], fromp.at[high], sems[1, 0], down)
+        send(table.at[high, :, b], fromm.at[high], sems[0, 1], up)
+        send(table.at[low, :, b], fromp.at[low], sems[1, 1], down)
 
     def ring_forward(fromm, fromp, far, sems, up, down):
         low, high = pl.ds(0, 2), pl.ds(2, 2)
@@ -283,7 +299,7 @@
 
     def zb_first(e, table):
         m, p, _, sems, up, down = zring(e)
-        ring_first(table, m, p, sems, up, down)
+        ring_first(table, cols_b[e], m, p, sems, up, down)
 
     def zb_forward(e):
         ring_forward(*zring(e))
@@ -302,21 +318,21 @@
 
         def wanted(row):
             want = reqs_s[row, 0, p]
-            return table[want, :, B] if r == 0 else table[want]
-
-        gbb[3 * r] = wanted(8)
-        send(gbb.at[3 * r], xfb.at[e, 0, r], xsb.at[e, 0, r], dev(xp, y, z, c))
-        gbb[3 * r + 1] = wanted(9)
-        send(gbb.at[3 * r + 1], xfb.at[e, 1, r], xsb.at[e, 1, r], dev(xm, y, z, c))
-        gbb[3 * r + 2] = wanted(z * 2 + 1 - c)
-        send(gbb.at[3 * r + 2], rbb.at[e, p], rpb.at[e, r], partner)
-        rbb[e, p] = wanted(z * 2 + c)
+            return table[want, :, cols_b[e]] if r == 0 else table[want]
+
+        gbb[e][3 * r] = wanted(8)
+        send(gbb[e].at[3 * r], xfb[e].at[0, r], xsb.at[e, 0, r], dev(xp, y, z, c))
+        gbb[e][3 * r + 1] = wanted(9)
+        send(gbb[e].at[3 * r + 1], xfb[e].at[1, r], xsb.at[e, 1, r], dev(xm, y, z, c))
+        gbb[e][3 * r + 2] = wanted(z * 2 + 1 - c)
+        send(gbb[e].at[3 * r + 2], rbb[e].at[p], rpb.at[e, r], partner)
+        rbb[e][p] = wanted(z * 2 + c)
 
     def xb_forward(e, r):
-        arrived(xfb.at[e, 0, r], xsb.at[e, 0, r])
-        send(xfb.at[e, 0, r], rbb.at[e, rel_z[r] * 4 + (xm // 2) * 2 + c], rsb.at[e, r, c], dev(xp, y, z, 0))
-        arrived(xfb.at[e, 1, r], xsb.at[e, 1, r])
-        send(xfb.at[e, 1, r], rbb.at[e, rel_z[r] * 4 + (xp // 2) * 2 + c], rsb.at[e, r, c], dev(xm, y, z, 1))
+        arrived(xfb[e].at[0, r], xsb.at[e, 0, r])
+        send(xfb[e].at[0, r], rbb[e].at[rel_z[r] * 4 + (xm // 2) * 2 + c], rsb.at[e, r, c], dev(xp, y, z, 0))
+        arrived(xfb[e].at[1, r], xsb.at[e, 1, r])
+        send(xfb[e].at[1, r], rbb[e].at[rel_z[r] * 4 + (xp // 2) * 2 + c], rsb.at[e, r, c], dev(xm, y, z, 1))
 
 
     def dot_into(total, lhs, rhs, start, width, first=False):
@@ -336,21 +352,21 @@
     def dot_a(e, ty, key):
         pz = (zm, zp, z2, z)[key]
         if key == 3:
-            arrived(rba.at[e, part(z, ty, 1 - c)], rsa.at[e, 3, ty, 0])
+            arrived(rba[e].at[part(z, ty, 1 - c)], rsa.at[e, 3, ty, 0])
         else:
             for pc in range(2):
-                arrived(rba.at[e, part(pz, ty, pc)], rsa.at[e, key, ty, pc])
+                arrived(rba[e].at[part(pz, ty, pc)], rsa.at[e, key, ty, pc])
         j = pz * 2 + (xh if ty == OWN else 1 - xh)
-        dot_into(acc, adj.at[2 + j], rba.at[e, pair(j)], 0, CA)
+        dot_into(acc, adj.at[2 + j], rba[e].at[pair(j)], 0, CA[e])
 
     def dot_b(e, ty, r):
         if ty == OWN:
-            arrived(rbb.at[e, part(rel_z[r], OWN, 1 - c)], rpb.at[e, r])
+            arrived(rbb[e].at[part(rel_z[r], OWN, 1 - c)], rpb.at[e, r])
         else:
             for pc in range(2):
-                arrived(rbb.at[e, part(rel_z[r], ANT, pc)], rsb.at[e, r, pc])
+                arrived(rbb[e].at[part(rel_z[r], ANT, pc)], rsb.at[e, r, pc])
         j = rel_z[r] * 2 + (xh if ty == OWN else 1 - xh)
-        dot_into(acc, adj.at[2 + j], rbb.at[e, pair(j)], CA, CB)
+        dot_into(acc, adj.at[2 + j], rbb[e].at[pair(j)], CA[e], CB[e])
 
     def layer(level, added, target, after=lambda half: None, blocks=True):
         beta = math.log(LAMBDA / level + 1.0)
@@ -425,6 +441,8 @@
         xb_first(e, 0, table)
 
     begin(0, init)
+    xa_forward(0, 0)
+    xa_forward(0, 1)
     zb_forward(0)
     za_rest(0, OWN, init)
     for py in (yp, ym, y2):
@@ -432,39 +450,36 @@
     arrived(xreqs.at[4], qsem.at[14])
     copy_xreq = pltpu.make_async_copy(xreqs, xreqs_s, lsem.at[7])
     copy_xreq.start()
-    copy_xreq.wait()
     copy_tbl.wait()
     loads["tiles0"].wait()
-    xa_forward(0, 0)
+    xb_forward(0, 0)
     zb_done(0)
     xb_first(0, 1)
     xb_first(0, 2)
-    chain(tiles, scale_ref, 0, 0, 32)
-    xa_forward(0, 1)
-    chain(tiles, scale_ref, 0, 32, 64)
+    chain(tiles, scale_ref, 0, 0, 48)
+    xa_done(0)
+    za_first(0, ANT, anta[0])
     za_forward(0, OWN)
-    xb_forward(0, 0)
+    za_rest(0, ANT, anta[0])
+    chain(tiles, scale_ref, 0, 48, 96)
     zb_far_done(0)
     xb_first(0, 3)
-    chain(tiles, scale_ref, 0, 64, 96)
-    loads["tiles1"].wait()
     xb_forward(0, 1)
     xb_forward(0, 2)
+    loads["tiles1"].wait()
     chain(tiles, scale_ref, 0, 96, 144)
-    xa_done(0)
-    za_first(0, ANT, anta[0])
-    za_rest(0, ANT, anta[0])
     xb_forward(0, 3)
     chain(tiles, scale_ref, 0, 144, 192)
     load("xtiles", xtiles_hbm, tiles.at[pl.ds(0, XTILES)], 8)
+    za_forward(0, ANT)
     place(adj, 0, SOURCES)
     dot_own(init)
-    za_forward(0, ANT)
     for key in (3, 0, 1, 2):
         dot_a(0, OWN, key)
     for r in range(4):
         dot_b(0, OWN, r)
         dot_b(0, ANT, r)
+    copy_xreq.wait()
     loads["held"].wait()
     loads["weights"].wait()
     for key in (3, 0, 1, 2):
@@ -476,33 +491,33 @@
     zb_first(1, h1)
     begin(1, h1)
     dot_own(h1)
+    xa_forward(1, 0)
+    xa_forward(1, 1)
     zb_forward(1)
     za_rest(1, OWN, h1)
-    xa_forward(1, 0)
+    xb_forward(1, 0)
+    dot_a(1, OWN, 3)
+    dot_b(1, OWN, 0)
     zb_done(1)
     xb_first(1, 1)
     xb_first(1, 2)
-    dot_a(1, OWN, 3)
-    dot_b(1, OWN, 0)
-    xa_forward(1, 1)
-    xb_forward(1, 0)
+    xa_done(1)
+    za_first(1, ANT, anta[1])
     za_forward(1, OWN)
+    za_rest(1, ANT, anta[1])
+    dot_b(1, OWN, 1)
+    dot_b(1, OWN, 2)
     zb_far_done(1)
     xb_first(1, 3)
-    dot_b(1, OWN, 1)
-    dot_b(1, OWN, 2)
-    dot_b(1, OWN, 3)
     xb_forward(1, 1)
     xb_forward(1, 2)
-    xa_done(1)
-    za_first(1, ANT, anta[1])
-    za_rest(1, ANT, anta[1])
-    xb_forward(1, 3)
+    dot_b(1, ANT, 0)
+    dot_b(1, OWN, 3)
     dot_a(1, OWN, 0)
     dot_a(1, OWN, 1)
+    xb_forward(1, 3)
     dot_a(1, OWN, 2)
     dot_a(1, ANT, 3)
-    dot_b(1, ANT, 0)
     za_forward(1, ANT)
     loads["xtiles"].wait()
     chain(tiles, xscale_ref, 1, 0, XTILES)
@@ -516,16 +531,29 @@
     h2 = hbuf.at[1]
 
     def na_first(half):
-        for k in range(2 * half, 2 * half + 2):
-            send(h2.at[k, :, A], nba.at[k], ns.at[k], dev(xnb, y, z, c))
+        a = cols_a[2]
+        if half == 0:
+            send(h2.at[0, :, a], xfo, os.at[0], dev(xot, y, z, c))
+            order = (1,)
+        else:
+            order = (2, 3, 0)
+        for k in order:
+            send(h2.at[k, :, a], nba.at[k], ns.at[k], dev(xnb, y, z, c))
 
     def na_forward(k):
         arrived(nba.at[k], ns.at[k])
         send(nba.at[k], anta[2].at[k], asa.at[2, k], dev(xot, y, z, c))
 
+    def no_forward():
+        arrived(xfo, os.at[0])
+        send(xfo, anta[2].at[0], asa.at[2, 0], dev(xnb, y, z, c))
+
+    def na_done():
+        arrived(nba.at[0], ns.at[0])
+
     def ya_gather(ty, table, g, py, k):
         want = xreqs_s[py, 1 + k, group(y, ty)]
-        gxa[ty, g] = table[want, :, A]
+        gxa[ty, g] = table[want, :, cols_a[2]]
 
     def ya_first(ty, table):
         ya_gather(ty, table, 0, y2, 0)
@@ -541,7 +569,7 @@
             send(gxa.at[ty, pair(1 + i)], mine, csa.at[i, ty], dev(x, py, z, c))
         for k in range(2):
             want = xreqs_s[y, 1 + k, group(y, ty)]
-            cra[group(y, ty) * 2 + k] = table[want, :, A]
+            cra[group(y, ty) * 2 + k] = table[want, :, cols_a[2]]
 
     def ya_forward(ty):
         arrived(yfa.at[0, ty], yss.at[0, ty])
@@ -558,7 +586,7 @@
         for k in range(2):
             for row, keep in ((4, False), (y, True)):
                 want = xreqs_s[row, 1 + k, g]
-                value = table[want, :, B] if r == 0 else table[want]
+                value = table[want, :, cols_b[2]] if r == 0 else table[want]
                 if keep:
                     crb[g * 2 + k] = value
                 else:
@@ -573,17 +601,17 @@
         if key == 2:
             arrived(cra.at[g * 2], csa.at[2, ty])
             arrived(cra.at[g * 2 + 1], csa.at[3, ty])
-        dot_into(xacc, xadj.at[g], cra.at[pair(g)], 0, CA, first)
+        dot_into(xacc, xadj.at[g], cra.at[pair(g)], 0, CA[2], first)
 
     def cross_b(ty, r, first=False):
         g = group(rel_y[r], ty)
         if ty == ANT:
             arrived(crb.at[pair(g)], csb.at[r])
-        dot_into(xacc, xadj.at[g], crb.at[pair(g)], CA, CB, first)
+        dot_into(xacc, xadj.at[g], crb.at[pair(g)], CA[2], CB[2], first)
 
     layer(2, held, h2, na_first)
     zb_first(2, h2)
-    ring_first(h2, yagm, yagp, ysems, dev(x, yp, z, c), dev(x, ym, z, c))
+    ring_first(h2, cols_b[2], yagm, yagp, ysems, dev(x, yp, z, c), dev(x, ym, z, c))
     za_first(2, OWN, h2)
     ya_first(OWN, h2)
     xb_first(2, 0, h2)
@@ -591,24 +619,25 @@
     ring_forward(*yring)
     za_rest(2, OWN, h2)
     ya_rest(OWN, h2)
-    na_forward(0)
+    na_forward(1)
+    no_forward()
     zb_done(2)
     xb_first(2, 1)
     xb_first(2, 2)
     yb_first(0)
-    na_forward(1)
+    na_forward(2)
     ring_done(yagm, yagp, ysems)
     yb_first(1)
     yb_first(2)
     dot_own(h2)
-    na_forward(2)
+    na_forward(3)
     za_forward(2, OWN)
     ya_forward(OWN)
     zb_far_done(2)
     xb_first(2, 3)
     ring_far_done(yagz, ysems)
     yb_first(3)
-    na_forward(3)
+    na_done()
     ya_first(ANT, nba)
     ya_rest(ANT, nba)
     xb_forward(2, 0)
@@ -646,6 +675,18 @@
     dot_a(2, ANT, 2)
     layer(3, ref_ref, out_ref, blocks=False)
     drain()
+
+
+def finish(a, b, to_a, to_b, held_a, held_b, sem):
+    ins = [pltpu.make_async_copy(a, held_a, sem.at[0]), pltpu.make_async_copy(b, held_b, sem.at[1])]
+    outs = [pltpu.make_async_copy(held_a, to_a, sem.at[2]), pltpu.make_async_copy(held_b, to_b, sem.at[3])]
+    for copy in ins:
+        copy.start()
+    for copy, out in zip(ins, outs):
+        copy.wait()
+        out.start()
+    for out in outs:
+        out.wait()
 
 
 def per_device(
@@ -686,34 +727,45 @@
             pltpu.VMEM((ROWS, D), F32),
             pltpu.VMEM((ROWS, D), BF),
             pltpu.VMEM((2, 4, BLOCK, D), BF),
-            pltpu.VMEM((3, 16, BLOCK, CA), BF),
-            pltpu.VMEM((3, 16, BLOCK, CB), BF),
-            pltpu.VMEM((4, BLOCK, CA), BF),
-            pltpu.VMEM((4, BLOCK, CA), BF),
-            pltpu.VMEM((4, BLOCK, CA), BF),
-            pltpu.VMEM((2, 2, 2, BLOCK, CA), BF),
-            pltpu.VMEM((3, 2, 2, BLOCK, CA), BF),
-            pltpu.VMEM((4, BLOCK, CB), BF),
-            pltpu.VMEM((4, BLOCK, CB), BF),
-            pltpu.VMEM((4, BLOCK, CB), BF),
-            pltpu.VMEM((4, BLOCK, CB), BF),
-            pltpu.VMEM((4, BLOCK, CB), BF),
-            pltpu.VMEM((4, BLOCK, CB), BF),
-            pltpu.VMEM((4, BLOCK, CB), BF),
-            pltpu.VMEM((4, BLOCK, CB), BF),
-            pltpu.VMEM((4, BLOCK, CB), BF),
-            pltpu.VMEM((3, 2, 4, BLOCK, CB), BF),
-            pltpu.VMEM((4, BLOCK, CA), BF),
-            pltpu.VMEM((2, 7, BLOCK, CA), BF),
-            pltpu.VMEM((12, BLOCK, CB), BF),
-            pltpu.VMEM((16, BLOCK, CA), BF),
-            pltpu.VMEM((16, BLOCK, CB), BF),
-            pltpu.VMEM((2, 2, BLOCK, CA), BF),
-            pltpu.VMEM((2, 6, BLOCK, CA), BF),
-            pltpu.VMEM((4, BLOCK, CB), BF),
-            pltpu.VMEM((4, BLOCK, CB), BF),
-            pltpu.VMEM((4, BLOCK, CB), BF),
-            pltpu.VMEM((8, BLOCK, CB), BF),
+            pltpu.VMEM((16, BLOCK, CA[0]), BF),
+            pltpu.VMEM((16, BLOCK, CA[1]), BF),
+            pltpu.VMEM((16, BLOCK, CA[2]), BF),
+            pltpu.VMEM((16, BLOCK, CB[0]), BF),
+            pltpu.VMEM((16, BLOCK, CB[1]), BF),
+            pltpu.VMEM((16, BLOCK, CB[2]), BF),
+            pltpu.VMEM((4, BLOCK, CA[0]), BF),
+            pltpu.VMEM((4, BLOCK, CA[1]), BF),
+            pltpu.VMEM((4, BLOCK, CA[2]), BF),
+            pltpu.VMEM((2, 2, 2, BLOCK, CA[0]), BF),
+            pltpu.VMEM((2, 2, BLOCK, CA[0]), BF),
+            pltpu.VMEM((2, 2, BLOCK, CA[1]), BF),
+            pltpu.VMEM((2, 2, BLOCK, CA[2]), BF),
+            pltpu.VMEM((4, BLOCK, CB[0]), BF),
+            pltpu.VMEM((4, BLOCK, CB[1]), BF),
+            pltpu.VMEM((4, BLOCK, CB[2]), BF),
+            pltpu.VMEM((4, BLOCK, CB[0]), BF),
+            pltpu.VMEM((4, BLOCK, CB[1]), BF),
+            pltpu.VMEM((4, BLOCK, CB[2]), BF),
+            pltpu.VMEM((4, BLOCK, CB[0]), BF),
+            pltpu.VMEM((4, BLOCK, CB[1]), BF),
+            pltpu.VMEM((4, BLOCK, CB[2]), BF),
+            pltpu.VMEM((2, 4, BLOCK, CB[0]), BF),
+            pltpu.VMEM((2, 4, BLOCK, CB[1]), BF),
+            pltpu.VMEM((2, 4, BLOCK, CB[2]), BF),
+            pltpu.VMEM((4, BLOCK, CA[2]), BF),
+            pltpu.VMEM((BLOCK, CA[2]), BF),
+            pltpu.VMEM((2, 7, BLOCK, CA[0]), BF),
+            pltpu.VMEM((2, 7, BLOCK, CA[2]), BF),
+            pltpu.VMEM((12, BLOCK, CB[0]), BF),
+            pltpu.VMEM((12, BLOCK, CB[2]), BF),
+            pltpu.VMEM((16, BLOCK, CA[2]), BF),
+            pltpu.VMEM((16, BLOCK, CB[2]), BF),
+            pltpu.VMEM((2, 2, BLOCK, CA[2]), BF),
+            pltpu.VMEM((2, 6, BLOCK, CA[2]), BF),
+            pltpu.VMEM((4, BLOCK, CB[2]), BF),
+            pltpu.VMEM((4, BLOCK, CB[2]), BF),
+            pltpu.VMEM((4, BLOCK, CB[2]), BF),
+            pltpu.VMEM((8, BLOCK, CB[2]), BF),
             pltpu.VMEM((4, BLOCK), I32),
             pltpu.VMEM((10, 4, BLOCK), I32),
             pltpu.VMEM((5, 4, BLOCK), I32),
@@ -734,6 +786,7 @@
             dma((3, 4, 2)),
             dma((3, 4)),
             dma((4,)),
+            dma((1,)),
             dma((2, 2)),
             dma((4, 2)),
             dma((3, 2)),
@@ -758,7 +811,13 @@
         cross_src[0],
         cross_dst[0],
     )
-    return out[0], out[1]
+    return pl.pallas_call(
+        finish,
+        out_shape=(table, table),
+        in_specs=[hbm, hbm],
+        out_specs=(hbm, hbm),
+        scratch_shapes=[pltpu.VMEM((ROWS, D), BF)] * 2 + [dma((4,))],
+    )(*out)
 
 
 def solution(mesh):

time: 96 us -> 88.9 us (0.926)
  local copies, waits for them, and re-layouts: 3.74 us -> 0 us
  Pallas kernels: 90.8 us -> 87.4 us
    pallas_call x1, Pallas kernels: 90.8 us -> 85.4 us  [per_device(): pl.pallas_call(kernel, out_shape=(table, table), in_specs=[hbm, hbm, hbm,...]
    unnamed x2 -> x0, local copies, waits for them, and re-layouts: 3.74 us -> none
    pallas_call x0 -> x1, Pallas kernels: none -> 2.04 us  [per_device(): pl.pallas_call(finish, out_shape=(table, table), in_specs=[hbm, hbm], out...]
where the time goes in v3:
time: 88.9 us; the launch traced here: 88.7 us
  Pallas kernels  87.4 us (98%)
  between operations  1.29 us (1%)
    pallas_call x1, Pallas kernels, per_device(): pl.pallas_call(kernel, out_shape=(table, table), in_specs=[hbm, hbm, hbm,...  85.4 us
    pallas_call x1, Pallas kernels, per_device(): pl.pallas_call(finish, out_shape=(table, table), in_specs=[hbm, hbm], out...  2.04 us

profile of v3, /device:TPU:0, one launch (start us, length us, event | category | flops | bytes accessed | tf_op | source)
XLA Modules:
  0.0 88.7 jit_solution(8570033088799351444)
XLA Ops:
  1.3 85.4 %shard_map.149 = (bf16[512,512]{1,0:T(8,128)(2,1)}, bf16[512,512]{1,0:T(8,128)(2,1)}) custom-call(bf16[4,128,512]{2,1,0:T(8,128)(2,1)} %bitcast.15, bf16[512,512]{1,0:T(8,128)(2,1)} %held_hbm.1, bf16[3,512,512]{2,1,0:T(8,128)(2,1)} %weights_hbm.1, s32[1,16]{1,0:T(1,128)} %bitcast.20, bf16[192,128,128]{2,1,0:T(8,128)(2,1)} %bitcast.13, f32[1,192]{1,0:T(1,128)} %bitcast.16, ...), custom_call_target="tpu_custom_call" | custom-call | tf_op jit(solution)/shard_map/pallas_call | solution.py:713
  86.7 2.0 %shard_map.150 = (bf16[512,512]{1,0:T(8,128)(2,1)}, bf16[512,512]{1,0:T(8,128)(2,1)}) custom-call(bf16[512,512]{1,0:T(8,128)(2,1)} %get-tuple-element.4.a, bf16[512,512]{1,0:T(8,128)(2,1)} %get-tuple-element.5.b), custom_call_target="tpu_custom_call" | custom-call | tf_op jit(solution)/shard_map/pallas_call | solution.py:814

commit v4 on v3

--- a/solution.py
+++ b/solution.py
@@ -64,6 +64,8 @@
     xscale_ref,
     xsrc_ref,
     xdst_ref,
+    out_hbm,
+    ref_hbm,
     out_ref,
     ref_ref,
     init,
@@ -189,16 +191,30 @@
         pl.semaphore_signal(barrier, inc=1, device_id=peer, device_id_type=MESH)
     rq[0:1, 0:16] = need_ref[...]
     rq[1:3, 0:8] = xneed_ref[...]
+
+    keys[...] = jnp.full((8, 256), -1, I32)
+    live = count_ref[0, 0]
+    at = lax.broadcasted_iota(I32, (1, TILES), 1)
+    keys[0:1, 0:TILES] = jnp.where(at < live, dst_ref[...] * SOURCES + src_ref[...], -1)
+    chain_tables(keys, tbl, 2, TILES, 0)
+    keys[0:1, 0:256] = jnp.full((1, 256), -1, I32)
+    keys[0:1, 0:XTILES] = xdst_ref[...] * XSOURCES + xsrc_ref[...]
+    chain_tables(keys, tbl, 1, TILES, 1)
+    copy_tbl = pltpu.make_async_copy(tbl, tbl_s, lsem.at[5])
+    copy_tbl.start()
+    slots[TILES] = jnp.zeros((BLOCK, BLOCK), F32)
+
     loads["init"].wait()
     pl.semaphore_wait(barrier, len(peers))
 
     sent = []
+    used = iter(range(240))
 
     def send(src, dst, sem, device):
         copy = pltpu.make_async_remote_copy(
             src_ref=src,
             dst_ref=dst,
-            send_sem=ssem.at[len(sent)],
+            send_sem=ssem.at[next(used)],
             recv_sem=sem,
             device_id=device,
             device_id_type=MESH,
@@ -216,10 +232,9 @@
             device_id_type=MESH,
         ).wait_recv()
 
-    def drain():
-        for copy in sent:
+    def drain(copies):
+        for copy in copies:
             copy.wait_send()
-        sent.clear()
 
     def part(pz, ty, pc):
         return pz * 4 + (xh if ty == OWN else 1 - xh) * 2 + pc
@@ -413,18 +428,6 @@
     zb_first(0, init)
     reqs[z * 2 + c] = rq[...]
     xreqs[y] = rq[...]
-
-    keys[...] = jnp.full((8, 256), -1, I32)
-    live = count_ref[0, 0]
-    at = lax.broadcasted_iota(I32, (1, TILES), 1)
-    keys[0:1, 0:TILES] = jnp.where(at < live, dst_ref[...] * SOURCES + src_ref[...], -1)
-    chain_tables(keys, tbl, 2, TILES, 0)
-    keys[0:1, 0:256] = jnp.full((1, 256), -1, I32)
-    keys[0:1, 0:XTILES] = xdst_ref[...] * XSOURCES + xsrc_ref[...]
-    chain_tables(keys, tbl, 1, TILES, 1)
-    copy_tbl = pltpu.make_async_copy(tbl, tbl_s, lsem.at[5])
-    copy_tbl.start()
-    slots[TILES] = jnp.zeros((BLOCK, BLOCK), F32)
 
     for pz in (zp, zm, z2):
         for pc in range(2):
@@ -484,11 +487,13 @@
     loads["weights"].wait()
     for key in (3, 0, 1, 2):
         dot_a(0, ANT, key)
-    drain()
+    old = list(sent)
+    sent.clear()
     layer(1, held, hbuf.at[0], lambda half: xa_first(1, hbuf.at[0], half))
 
     h1 = hbuf.at[0]
     zb_first(1, h1)
+    drain(old)
     begin(1, h1)
     dot_own(h1)
     xa_forward(1, 0)
@@ -526,7 +531,8 @@
         dot_b(1, ANT, r)
     for key in (0, 1, 2):
         dot_a(1, ANT, key)
-    drain()
+    old = list(sent)
+    sent.clear()
 
     h2 = hbuf.at[1]
 
@@ -611,6 +617,7 @@
 
     layer(2, held, h2, na_first)
     zb_first(2, h2)
+    drain(old)
     ring_first(h2, cols_b[2], yagm, yagp, ysems, dev(x, yp, z, c), dev(x, ym, z, c))
     za_first(2, OWN, h2)
     ya_first(OWN, h2)
@@ -649,13 +656,13 @@
     xa_done(2)
     za_first(2, ANT, anta[2])
     za_rest(2, ANT, anta[2])
-    xb_forward(2, 3)
     for key in (3, 0, 1):
         dot_a(2, OWN, key)
     cross_a(OWN, 0)
     cross_a(OWN, 1)
     ya_forward(ANT)
     za_forward(2, ANT)
+    xb_forward(2, 3)
     for r in range(1, 4):
         cross_b(OWN, r)
     dot_a(2, OWN, 2)
@@ -672,9 +679,19 @@
     dot_a(2, ANT, 1)
     cross_a(ANT, 2)
     ref_ref[...] = xacc[...].astype(BF)
+    outs = [pltpu.make_async_copy(ref_ref, ref_hbm, lsem.at[9])]
+    outs[0].start()
     dot_a(2, ANT, 2)
-    layer(3, ref_ref, out_ref, blocks=False)
-    drain()
+
+    def write(half):
+        rows = pl.ds(half * 256, 256)
+        outs.append(pltpu.make_async_copy(out_ref.at[rows], out_hbm.at[rows], lsem.at[10 + half]))
+        outs[-1].start()
+
+    layer(3, ref_ref, out_ref, write, blocks=False)
+    drain(sent)
+    for copy in outs:
+        copy.wait()
 
 
 def finish(a, b, to_a, to_b, held_a, held_b, sem):
@@ -714,8 +731,10 @@
         kernel,
         out_shape=(table, table),
         in_specs=[hbm, hbm, hbm, vmem, hbm, smem, vmem, vmem, smem, vmem, hbm, smem, vmem, vmem],
-        out_specs=(vmem, vmem),
+        out_specs=(hbm, hbm),
         scratch_shapes=[
+            pltpu.VMEM((ROWS, D), BF),
+            pltpu.VMEM((ROWS, D), BF),
             pltpu.VMEM((4, BLOCK, D), BF),
             pltpu.VMEM((ROWS, D), BF),
             pltpu.VMEM((3, D, D), BF),
@@ -774,8 +793,8 @@
             pltpu.VMEM((8, 2 * BLOCK), I32),
             pltpu.VMEM((8, 3 * BLOCK), I32),
             pltpu.SMEM((8, 3 * BLOCK), I32),
-            dma((9,)),
-            dma((96,)),
+            dma((12,)),
+            dma((240,)),
             dma((15,)),
             dma((2, 2, 2)),
             dma((3, 4)),

time: 88.9 us -> 88.5 us (level)
  no operation moved by 1% of the time
where the time goes in v4:
time: 88.5 us; the launch traced here: 88.4 us
  Pallas kernels  87.1 us (98%)
  between operations  1.29 us (1%)
    pallas_call x1, Pallas kernels, per_device(): pl.pallas_call(kernel, out_shape=(table, table), in_specs=[hbm, hbm, hbm,...  85 us
    pallas_call x1, Pallas kernels, per_device(): pl.pallas_call(finish, out_shape=(table, table), in_specs=[hbm, hbm], out...  2.04 us

profile of v4, /device:TPU:0, one launch (start us, length us, event | category | flops | bytes accessed | tf_op | source)
XLA Modules:
  0.0 88.4 jit_solution(17386975479349420773)
XLA Ops:
  1.3 85.0 %shard_map.149 = (bf16[512,512]{1,0:T(8,128)(2,1)}, bf16[512,512]{1,0:T(8,128)(2,1)}) custom-call(bf16[4,128,512]{2,1,0:T(8,128)(2,1)} %bitcast.15, bf16[512,512]{1,0:T(8,128)(2,1)} %held_hbm.1, bf16[3,512,512]{2,1,0:T(8,128)(2,1)} %weights_hbm.1, s32[1,16]{1,0:T(1,128)} %bitcast.20, bf16[192,128,128]{2,1,0:T(8,128)(2,1)} %bitcast.13, f32[1,192]{1,0:T(1,128)} %bitcast.16, ...), custom_call_target="tpu_custom_call" | custom-call | tf_op jit(solution)/shard_map/pallas_call | solution.py:730
  86.3 2.0 %shard_map.150 = (bf16[512,512]{1,0:T(8,128)(2,1)}, bf16[512,512]{1,0:T(8,128)(2,1)}) custom-call(bf16[512,512]{1,0:T(8,128)(2,1)} %get-tuple-element.4.a, bf16[512,512]{1,0:T(8,128)(2,1)} %get-tuple-element.5.b), custom_call_target="tpu_custom_call" | custom-call | tf_op jit(solution)/shard_map/pallas_call | solution.py:833

commit v5 on v4

--- a/solution.py
+++ b/solution.py
@@ -185,7 +185,7 @@
     barrier = pltpu.get_barrier_semaphore()
     column = [dev(x, y, pz, pc) for pz in (zp, zm, z2) for pc in range(2)]
     across = [dev(x2, y, z, pc) for pc in range(2)]
-    peers = [dev(xp, y, z, 0), dev(xp, y, z, 1), dev(xm, y, z, 0), dev(xm, y, z, 1), partner] + column + across
+    peers = [dev(xp, y, z, c), dev(xm, y, z, c), dev((x + 3 - 2 * c) % 4, y, z, 1 - c), partner] + column + across
     peers += [dev(x, py, z, c) for py in (yp, ym, y2)]
     for peer in peers:
         pl.semaphore_signal(barrier, inc=1, device_id=peer, device_id_type=MESH)

time: 88.5 us -> 88.5 us (level)
  no operation moved by 1% of the time
where the time goes in v5:
time: 88.5 us; the launch traced here: 88.4 us
  Pallas kernels  87.1 us (98%)
  between operations  1.29 us (1%)
    pallas_call x1, Pallas kernels, per_device(): pl.pallas_call(kernel, out_shape=(table, table), in_specs=[hbm, hbm, hbm,...  85.1 us
    pallas_call x1, Pallas kernels, per_device(): pl.pallas_call(finish, out_shape=(table, table), in_specs=[hbm, hbm], out...  2.04 us

profile of v5, /device:TPU:0, one launch (start us, length us, event | category | flops | bytes accessed | tf_op | source)
XLA Modules:
  0.0 88.4 jit_solution(12777852022412060618)
XLA Ops:
  1.3 85.1 %shard_map.149 = (bf16[512,512]{1,0:T(8,128)(2,1)}, bf16[512,512]{1,0:T(8,128)(2,1)}) custom-call(bf16[4,128,512]{2,1,0:T(8,128)(2,1)} %bitcast.15, bf16[512,512]{1,0:T(8,128)(2,1)} %held_hbm.1, bf16[3,512,512]{2,1,0:T(8,128)(2,1)} %weights_hbm.1, s32[1,16]{1,0:T(1,128)} %bitcast.20, bf16[192,128,128]{2,1,0:T(8,128)(2,1)} %bitcast.13, f32[1,192]{1,0:T(1,128)} %bitcast.16, ...), custom_call_target="tpu_custom_call" | custom-call | tf_op jit(solution)/shard_map/pallas_call | solution.py:730
  86.3 2.0 %shard_map.150 = (bf16[512,512]{1,0:T(8,128)(2,1)}, bf16[512,512]{1,0:T(8,128)(2,1)}) custom-call(bf16[512,512]{1,0:T(8,128)(2,1)} %get-tuple-element.4.a, bf16[512,512]{1,0:T(8,128)(2,1)} %get-tuple-element.5.b), custom_call_target="tpu_custom_call" | custom-call | tf_op jit(solution)/shard_map/pallas_call | solution.py:833
